TPU v7x, 32 devices: a whole 2x2x4 slice. The times are simulated.
32 devices in a mesh: wide: 16 (over z, y, core), narrow: 2 (over x).
Axes of the slice: x: 2, y: 2, z: 4, core: 2. Of those that a mesh axis runs over, the one named last changes fastest.
Arguments:
- src_field: bfloat16 [2, 16, 65536], P(None, 'narrow', 'wide'), may hold values from -6 to 6
- src_depth: int32 [65536], P(('wide', 'narrow')), may hold values from 0 to 16, as said below
- packed_counts: int32 [4096, 64, 128], P(('wide', 'narrow')), may hold values from 0 to 100664832, as said below
- pair_source: int32 [4096], P(('wide', 'narrow')), may hold values from 0 to 15
- pair_home: int32 [4096], P(('wide', 'narrow')), may hold values from 0 to 1023, as said below
- pair_count: int32 [32], P(('wide', 'narrow')), may hold values from 64 to 128, as said below
Outputs:
- remapped: bfloat16 [2, 16, 131072], P(None, 'narrow', 'wide')
Inputs may be any that keep to these rules, and one draw needn't show every extreme that they name: `src_depth`: depth 0 marks a dry source cell. `packed_counts`: word (p, i, j) holds count (p, i, j) plus 65536 times count (p, i + 64, j); every count lies between 0 and 1536. The target block pair_home[p] is held by wide index pair_home[p] // 64, which differs by at most 2, counted cyclically over the wide axis, from the wide index of the device that holds pair p. Among the 128 pairs of one device at most 51 have target blocks on one wide index, and on some wide index exactly 51 live pairs of that device. A device's pairs from position pair_count[d] on are padding; some device has all 128 live.
All inputs are finite; a program needn't handle non-finite values.
Results may differ from a plain program's by a relative error of at most 0.0054.
Values may be sent and summed in bfloat16 or wider, within the bound.
No kernel may reach another device: no remote copies, remote signals or barrier semaphores. Data moves between devices by JAX's collectives and lax.ppermute only.
A program may use at most 64 MiB of HBM per device.

v0:
```python
import jax
import jax.numpy as jnp
from jax import lax
from jax.sharding import PartitionSpec as P

DENOM = 256
REACH = 2
TB_DEV = 64


wet_limit = 0.001


def passed_along(block, axis, distance):
    devices = range(lax.axis_size(axis))
    route = [((i - distance) % len(devices), i) for i in devices]
    return lax.ppermute(block, axis, route)


def unpack_counts(packed_words):
    return jnp.concatenate([packed_words % 65536, packed_words // 65536], axis=-2)


def block_sums(targets, received, block_count):
    owners = jnp.arange(block_count, dtype=jnp.int32)
    select = (targets[:, None] == owners[None, :]).astype(jnp.bfloat16)
    return jnp.einsum("rq,rlcb->lcqb", select, received, preferred_element_type=jnp.float32)


def per_device(src_field, src_depth, packed_counts, pair_source, pair_home, pair_count):
    narrow_size = lax.axis_size("narrow")
    wide_size = lax.axis_size("wide")
    field_vars = src_field.shape[0]
    components = field_vars + 1
    block_cells = packed_counts.shape[2]
    own_cells = src_depth.shape[0]
    own_tiles = own_cells // block_cells
    pair_slots = pair_source.shape[0]
    offset_count = 2 * REACH + 1
    capacity = max(2, 2 * pair_slots // offset_count)
    own_field = lax.all_to_all(src_field, "narrow", split_axis=2, concat_axis=1, tiled=True)
    levels = own_field.shape[1]
    part_levels = levels // narrow_size
    level_ids = jnp.arange(levels, dtype=jnp.int32)
    wet_levels = level_ids[:, None] < src_depth[None, :]
    masked = jnp.where(wet_levels[None, :, :], own_field, jnp.zeros_like(own_field))
    stacked = jnp.concatenate(
        [jnp.transpose(masked, (1, 0, 2)), wet_levels.astype(jnp.bfloat16)[:, None, :]], axis=1
    )
    by_tile = jnp.transpose(stacked.reshape(levels * components, own_tiles, block_cells), (1, 0, 2))
    picked = jnp.take(by_tile, pair_source, axis=0)
    weight = (unpack_counts(packed_counts).astype(jnp.float32) / DENOM).astype(jnp.bfloat16)
    pair_terms = lax.dot_general(
        picked, weight, (((2,), (2,)), ((0,), (0,))), preferred_element_type=jnp.float32
    )
    pair_terms = pair_terms.astype(jnp.bfloat16)
    is_live = jnp.arange(pair_slots, dtype=jnp.int32) < pair_count[0]
    wide_index = lax.axis_index("wide")
    destination = pair_home // TB_DEV
    local_block = pair_home % TB_DEV
    offset_index = (destination - wide_index + REACH + wide_size) % wide_size
    bound_for = (
        (offset_index[:, None] == jnp.arange(offset_count, dtype=jnp.int32)[None, :])
        & is_live[:, None]
    ).astype(jnp.int32)
    before = jnp.cumsum(bound_for, axis=0) - bound_for
    position = jnp.sum(before * bound_for, axis=1)
    slot_index = jnp.where(is_live, offset_index * capacity + position, offset_count * capacity)
    outgoing = (
        jnp.zeros((offset_count * capacity, levels * components, block_cells), jnp.bfloat16)
        .at[slot_index]
        .set(pair_terms, mode="drop")
    )
    targets = (
        jnp.full((offset_count * capacity,), TB_DEV, jnp.int32)
        .at[slot_index]
        .set(local_block, mode="drop")
    )
    outgoing = outgoing.reshape(offset_count, capacity, levels, components, block_cells)
    targets = targets.reshape(offset_count, capacity)
    shift_list = [shift_by for shift_by in range(-REACH, REACH + 1) if shift_by != 0]
    partial_value = block_sums(targets[REACH], outgoing[REACH], TB_DEV)
    for shift_by in shift_list:
        moved_terms, moved_owners = passed_along(
            (outgoing[REACH + shift_by], targets[REACH + shift_by]), "wide", shift_by
        )
        partial_value = partial_value + block_sums(moved_owners, moved_terms, TB_DEV)
    block_totals = lax.psum_scatter(partial_value, "narrow", scatter_dimension=0, tiled=True)
    numerators = block_totals[:, :field_vars]
    wet_total = block_totals[:, field_vars]
    covered = wet_total > wet_limit
    safe_wet = jnp.where(covered, wet_total, jnp.ones_like(wet_total))
    result = jnp.where(covered[:, None], numerators / safe_wet[:, None], jnp.zeros_like(numerators))
    result = jnp.transpose(result, (1, 0, 2, 3)).reshape(
        field_vars, part_levels, TB_DEV * block_cells
    )
    return result.astype(jnp.bfloat16)


def solution(mesh):
    placed = (
        P(None, "narrow", "wide"),
        P(("wide", "narrow")),
        P(("wide", "narrow"), None, None),
        P(("wide", "narrow")),
        P(("wide", "narrow")),
        P(("wide", "narrow")),
    )
    return jax.shard_map(
        per_device, mesh=mesh, in_specs=placed, out_specs=P(None, "narrow", "wide"), check_vma=False
    )
```

profile of v0, /device:TPU:0, one launch (start us, length us, event | category | flops | bytes accessed | tf_op | source)
XLA Modules:
  0.0 141.6 jit_solution(15521793403621437424)
XLA Ops:
  6.5 4.4 %copy.29 = bf16[2,8,4096]{1,0,2:T(2,128)(2,1)S(1)} copy(bf16[2,8,4096]{2,1,0:T(8,128)(2,1)} %param.6) | data formatting | bytes 262144 | tf_op args[0]
  10.9 2.8 %reshape.126 = bf16[2,2,16384]{2,1,0:T(2,128)(2,1)} reshape(bf16[4096,2,8]{2,1,0:T(2,128)(2,1)S(1)} %bitcast.60) | data formatting | bytes 262144
  13.8 4.2 %all-to-all-start = ((bf16[2,2,16384]{2,1,0:T(2,128)(2,1)}), bf16[2,2,16384]{2,1,0:T(2,128)(2,1)S(1)}, u32[]{:S(2)}, u32[]{:S(2)}) async-start(bf16[2,2,16384]{2,1,0:T(2,128)(2,1)} %reshape.126), calls=%async_computation | async-start | bytes 262144 | tf_op jit(solution)/shard_map/all_to_all | solution.py:41
  18.0 0.1 compare_convert_fusion
  18.9 0.1 fusion.29
  19.0 0.2 reduce_window_sum.11
  19.2 0.2 select_reduce_fusion
  19.4 7.1 %add_select_fusion.1 = (s32[128,64,128]{2,1,0:T(8,128)}, s32[128,64,128]{2,1,0:T(8,128)}) fusion(s32[128,64,128]{2,1,0:T(8,128)} %param.8), kind=kLoop, calls=%fused_computation.8 | loop fusion | flops 19922944 | bytes 12582912 | tf_op jit(solution)/shard_map/jit(remainder)/select_n | solution.py:21
  26.5 2.5 %reshape.127 = bf16[4096,2,8]{2,1,0:T(2,128)(2,1)S(1)} reshape(bf16[2,2,16384]{2,1,0:T(2,128)(2,1)S(1)} %all-to-all-done) | data formatting | bytes 262144
  28.9 1.4 copy.30
  30.3 0.2 fusion.27
  30.6 0.3 pad_maximum_fusion
  30.9 0.2 reshape.91
  31.1 0.9 gather_fusion
  32.0 7.7 %fusion.7 = bf16[128,48,128]{2,1,0:T(8,128)(2,1)} fusion(s32[128,64,128]{2,1,0:T(8,128)} %get-tuple-element.6, s32[128,64,128]{2,1,0:T(8,128)} %get-tuple-element.5, bf16[128,48,128]{2,1,0:T(8,128)(2,1)S(1)} %gather_fusion, pred[128]{0:T(512)(128)(4,1)S(1)} %compare_and_fusion), kind=kOutput, calls=%fused_computation.16 | convolution fusion | flops 211288064 | bytes 11534464 | tf_op jit(solution)/shard_map/dot_general | solution.py:53
  39.7 0.4 broadcast_in_dim.71
  40.2 11.7 %scatter_fusion = bf16[255,48,128]{2,1,0:T(8,128)(2,1)S(1)} fusion(bf16[255,48,128]{2,1,0:T(8,128)(2,1)S(1)} %broadcast_in_dim.71, s32[128]{0:T(128)S(1)} %compare_select_fusion.2, bf16[128,48,128]{2,1,0:T(8,128)(2,1)} %fusion.7), kind=kCustom, calls=%fused_computation.1 | custom fusion | bytes 4719104 | tf_op jit(solution)/shard_map/scatter | solution.py:72
  51.9 1.7 %fusion.52 = (bf16[51,48,128]{2,1,0:T(8,128)(2,1)}, bf16[51,48,128]{2,1,0:T(8,128)(2,1)}, bf16[51,48,128]{2,1,0:T(8,128)(2,1)S(1)}, bf16[51,48,128]{2,1,0:T(8,128)(2,1)}, bf16[51,48,128]{2,1,0:T(8,128)(2,1)}) fusion(bf16[255,48,128]{2,1,0:T(8,128)(2,1)S(1)} %scatter_fusion), kind=kLoop, calls=%fused_computation.81 | loop fusion | bytes 6266880 | tf_op jit(solution)/shard_map/slice | solution.py:85
  53.6 0.2 copy.36
  53.8 0.1 copy.37
  53.9 4.8 %collective-permute-start.2 = (bf16[51,16,3,128]{3,1,2,0:T(8,128)(2,1)S(1)}, bf16[51,16,3,128]{3,1,2,0:T(8,128)(2,1)S(1)}, u32[]{:S(2)}, u32[]{:S(2)}) collective-permute-start(bf16[51,16,3,128]{3,1,2,0:T(8,128)(2,1)S(1)} %copy.37), channel_id=1, source_target_pairs={{2,0},{4,2},{6,4},{8,6},{10,8},{12,10},{14,12},{16,14},{18,16},{20... | collective-permute-start | bytes 1880072 | tf_op jit(solution)/shard_map/ppermute | solution.py:17
  58.7 1.0 scatter_custom_fusion.1
  59.7 1.2 copy.33
  60.9 0.1 copy.34
  61.0 0.6 collective-permute-start
  61.7 0.1 fusion.53
  61.8 0.3 collective-permute-start.3
  62.0 1.4 %collective-permute-start.1 = (s32[51]{0:T(128)S(1)}, s32[51]{0:T(128)S(1)}, u32[]{:S(2)}, u32[]{:S(2)}) collective-permute-start(s32[51]{0:T(128)S(1)} %get-tuple-element.15), channel_id=1, source_target_pairs={{4,0},{6,2},{8,4},{10,6},{12,8},{14,10},{16,12},{18,14},{20,16},{2... | collective-permute-start | bytes 620 | tf_op jit(solution)/shard_map/ppermute | solution.py:17
  63.5 0.2 copy.39
  63.7 0.1 copy.40
  63.7 0.2 collective-permute-start.4
  64.0 0.2 copy.32
  64.2 0.5 fusion.31
  64.7 0.2 copy.42
  64.9 0.1 copy.43
  65.0 15.0 %collective-permute-done.3 = s32[51]{0:T(128)S(1)} collective-permute-done((s32[51]{0:T(128)S(1)}, s32[51]{0:T(128)S(1)}, u32[]{:S(2)}, u32[]{:S(2)}) %collective-permute-start.3) | collective-permute-done | bytes 236 | tf_op jit(solution)/shard_map/ppermute | solution.py:17
  80.0 4.8 %collective-permute-start.5 = (s32[51]{0:T(128)S(1)}, s32[51]{0:T(128)S(1)}, u32[]{:S(2)}, u32[]{:S(2)}) collective-permute-start(s32[51]{0:T(128)S(1)} %get-tuple-element.13), channel_id=1, source_target_pairs={{30,0},{0,2},{2,4},{4,6},{6,8},{8,10},{10,12},{12,14},{14,16},{16,... | collective-permute-start | bytes 620 | tf_op jit(solution)/shard_map/ppermute | solution.py:17
  84.8 0.5 fusion.19
  85.3 3.1 %collective-permute-start.7 = (s32[51]{0:T(128)S(1)}, s32[51]{0:T(128)S(1)}, u32[]{:S(2)}, u32[]{:S(2)}) collective-permute-start(s32[51]{0:T(128)S(1)} %get-tuple-element.12), channel_id=1, source_target_pairs={{28,0},{30,2},{0,4},{2,6},{4,8},{6,10},{8,12},{10,14},{12,16},{14,... | collective-permute-start | bytes 620 | tf_op jit(solution)/shard_map/ppermute | solution.py:17
  88.3 0.5 fusion.21
  88.9 0.5 fusion.17
  89.3 14.3 %collective-permute-done.7 = s32[51]{0:T(128)S(1)} collective-permute-done((s32[51]{0:T(128)S(1)}, s32[51]{0:T(128)S(1)}, u32[]{:S(2)}, u32[]{:S(2)}) %collective-permute-start.7) | collective-permute-done | bytes 236 | tf_op jit(solution)/shard_map/ppermute | solution.py:17
  103.6 1.8 %add_bitcast_fusion = f32[16,3,64,128]{3,2,1,0:T(8,128)} fusion(f32[16,3,128,64]{2,3,1,0:T(8,128)S(1)} %fusion.17, f32[16,3,128,64]{2,3,1,0:T(8,128)S(1)} %fusion.19, f32[16,3,128,64]{2,3,1,0:T(8,128)S(1)} %fusion.31, f32[16,3,128,64]{2,3,1,0:T(8,128)S(1)} %fusion.21, bf16[51,16,3,128]{3,1,2,0:T(8,128)(2,1)S(1)} %collective-permute-done.6, ...), kind=kOutput, calls=%fused_computation.17 | convolution fusion | flops 41684160 | bytes 8491212 | tf_op jit(solution)/shard_map/rq,rlcb->lcqb/dot_general | solution.py:27
  105.5 25.3 %reduce-scatter.2.cloned.1.call-done = f32[8,3,64,128]{3,2,1,0:T(8,128)} async-done(((f32[16,3,64,128]{3,2,1,0:T(8,128)}), f32[8,3,64,128]{3,2,1,0:T(8,128)}) %reduce-scatter.2.cloned.1.call-update) | async-done | bytes 786448 | tf_op jit(solution)/shard_map/reduce_scatter | solution.py:88
  130.7 1.0 fusion.25
  131.7 1.0 compare_bitcast_fusion
  132.7 1.1 fusion.26
  133.9 0.9 copy.45
  (31 shorter events, 0.3 us)
Async XLA Ops:
  6.5 11.5 %copy-start.3 = (s32[2048]{0:T(1024)S(1)}, s32[2048]{0:T(1024)}, u32[]{:S(2)}) copy-start(s32[2048]{0:T(1024)} %param.7) | copy-start | bytes 24580
  6.5 11.6 %copy-start.5 = (s32[128]{0:T(128)S(1)}, s32[128]{0:T(128)}, u32[]{:S(2)}) copy-start(s32[128]{0:T(128)} %param.9) | copy-start | bytes 1540
  6.5 12.3 %copy-start.4 = (s32[128]{0:T(128)S(1)}, s32[128]{0:T(128)}, u32[]{:S(2)}) copy-start(s32[128]{0:T(128)} %param.10) | copy-start | bytes 1540
  13.8 12.7 %all-to-all-start = ((bf16[2,2,16384]{2,1,0:T(2,128)(2,1)}), bf16[2,2,16384]{2,1,0:T(2,128)(2,1)S(1)}, u32[]{:S(2)}, u32[]{:S(2)}) async-start(bf16[2,2,16384]{2,1,0:T(2,128)(2,1)} %reshape.126), calls=%async_computation | async-start | bytes 262144 | tf_op jit(solution)/shard_map/all_to_all | solution.py:41
  18.0 112.7 %reduce-scatter.2.cloned.1.call-start = ((), (), s32[]{:S(2)}) async-start(), calls=%async_computation.2 | async-start | bytes 2359296 | tf_op jit(solution)/shard_map/reduce_scatter | solution.py:88
  53.6 9.8 %copy-start.2 = (bf16[51,48,128]{2,1,0:T(8,128)(2,1)S(1)}, bf16[51,48,128]{2,1,0:T(8,128)(2,1)}, u32[]{:S(2)}) copy-start(bf16[51,48,128]{2,1,0:T(8,128)(2,1)} %get-tuple-element.8) | copy-start | bytes 1880068
  53.8 10.2 %copy-start.1 = (bf16[51,48,128]{2,1,0:T(8,128)(2,1)S(1)}, bf16[51,48,128]{2,1,0:T(8,128)(2,1)}, u32[]{:S(2)}) copy-start(bf16[51,48,128]{2,1,0:T(8,128)(2,1)} %get-tuple-element.11) | copy-start | bytes 1880068
  53.9 30.9 %collective-permute-start.2 = (bf16[51,16,3,128]{3,1,2,0:T(8,128)(2,1)S(1)}, bf16[51,16,3,128]{3,1,2,0:T(8,128)(2,1)S(1)}, u32[]{:S(2)}, u32[]{:S(2)}) collective-permute-start(bf16[51,16,3,128]{3,1,2,0:T(8,128)(2,1)S(1)} %copy.37), channel_id=1, source_target_pairs={{2,0},{4,2},{6,4},{8,6},{10,8},{12,10},{14,12},{16,14},{18,16},{20... | collective-permute-start | bytes 1880072 | tf_op jit(solution)/shard_map/ppermute | solution.py:17
  61.0 3.6 %copy-start = (bf16[51,48,128]{2,1,0:T(8,128)(2,1)S(1)}, bf16[51,48,128]{2,1,0:T(8,128)(2,1)}, u32[]{:S(2)}) copy-start(bf16[51,48,128]{2,1,0:T(8,128)(2,1)} %get-tuple-element.7) | copy-start | bytes 1880068
  61.0 27.3 %collective-permute-start = (bf16[51,16,3,128]{3,1,2,0:T(8,128)(2,1)S(1)}, bf16[51,16,3,128]{3,1,2,0:T(8,128)(2,1)S(1)}, u32[]{:S(2)}, u32[]{:S(2)}) collective-permute-start(bf16[51,16,3,128]{3,1,2,0:T(8,128)(2,1)S(1)} %copy.34), channel_id=1, source_target_pairs={{4,0},{6,2},{8,4},{10,6},{12,8},{14,10},{16,12},{18,14},{20,16},{2... | collective-permute-start | bytes 1880072 | tf_op jit(solution)/shard_map/ppermute | solution.py:17
  61.8 18.2 %collective-permute-start.3 = (s32[51]{0:T(128)S(1)}, s32[51]{0:T(128)S(1)}, u32[]{:S(2)}, u32[]{:S(2)}) collective-permute-start(s32[51]{0:T(128)S(1)} %get-tuple-element.14), channel_id=1, source_target_pairs={{2,0},{4,2},{6,4},{8,6},{10,8},{12,10},{14,12},{16,14},{18,16},{20... | collective-permute-start | bytes 620 | tf_op jit(solution)/shard_map/ppermute | solution.py:17
  62.0 23.2 %collective-permute-start.1 = (s32[51]{0:T(128)S(1)}, s32[51]{0:T(128)S(1)}, u32[]{:S(2)}, u32[]{:S(2)}) collective-permute-start(s32[51]{0:T(128)S(1)} %get-tuple-element.15), channel_id=1, source_target_pairs={{4,0},{6,2},{8,4},{10,6},{12,8},{14,10},{16,12},{18,14},{20,16},{2... | collective-permute-start | bytes 620 | tf_op jit(solution)/shard_map/ppermute | solution.py:17
  63.7 25.1 %collective-permute-start.4 = (bf16[51,16,3,128]{3,1,2,0:T(8,128)(2,1)S(1)}, bf16[51,16,3,128]{3,1,2,0:T(8,128)(2,1)S(1)}, u32[]{:S(2)}, u32[]{:S(2)}) collective-permute-start(bf16[51,16,3,128]{3,1,2,0:T(8,128)(2,1)S(1)} %copy.40), channel_id=1, source_target_pairs={{30,0},{0,2},{2,4},{4,6},{6,8},{8,10},{10,12},{12,14},{14,16},{16,... | collective-permute-start | bytes 1880072 | tf_op jit(solution)/shard_map/ppermute | solution.py:17
  80.0 8.9 %collective-permute-start.5 = (s32[51]{0:T(128)S(1)}, s32[51]{0:T(128)S(1)}, u32[]{:S(2)}, u32[]{:S(2)}) collective-permute-start(s32[51]{0:T(128)S(1)} %get-tuple-element.13), channel_id=1, source_target_pairs={{30,0},{0,2},{2,4},{4,6},{6,8},{8,10},{10,12},{12,14},{14,16},{16,... | collective-permute-start | bytes 620 | tf_op jit(solution)/shard_map/ppermute | solution.py:17
  84.8 18.8 %collective-permute-start.6 = (bf16[51,16,3,128]{3,1,2,0:T(8,128)(2,1)S(1)}, bf16[51,16,3,128]{3,1,2,0:T(8,128)(2,1)S(1)}, u32[]{:S(2)}, u32[]{:S(2)}) collective-permute-start(bf16[51,16,3,128]{3,1,2,0:T(8,128)(2,1)S(1)} %copy.43), channel_id=1, source_target_pairs={{28,0},{30,2},{0,4},{2,6},{4,8},{6,10},{8,12},{10,14},{12,16},{14,... | collective-permute-start | bytes 1880072 | tf_op jit(solution)/shard_map/ppermute | solution.py:17
  85.3 18.3 %collective-permute-start.7 = (s32[51]{0:T(128)S(1)}, s32[51]{0:T(128)S(1)}, u32[]{:S(2)}, u32[]{:S(2)}) collective-permute-start(s32[51]{0:T(128)S(1)} %get-tuple-element.12), channel_id=1, source_target_pairs={{28,0},{30,2},{0,4},{2,6},{4,8},{6,10},{8,12},{10,14},{12,16},{14,... | collective-permute-start | bytes 620 | tf_op jit(solution)/shard_map/ppermute | solution.py:17
Sparse Core Ops, SparseCore 0:
  105.6 25.0 reduce-scatter.1
where the time goes:
time: 142 us
  waiting for transfers between devices  54.6 us (38%)
  local copies, waits for them, and re-layouts  30.3 us (21%)
  starting transfers between devices  19.5 us (14%)
  between operations  14.4 us (10%)
  matrix products  11.5 us (8%)
  other arithmetic  11.4 us (8%)
    ppermute x8, waiting for transfers between devices, passed_along(): return lax.ppermute(block, axis, route)  29.3 us
    reduce_scatter x1, waiting for transfers between devices, per_device(): lax.psum_scatter(partial_value, 'narrow', scatter_dimension=0, tiled=True)  25.3 us
    ppermute x8, starting transfers between devices, passed_along(): return lax.ppermute(block, axis, route)  15.3 us
    scatter x1, local copies, waits for them, and re-layouts, per_device(): outgoing = jnp.zeros((offset_count * capacity, levels * components, block...  11.7 us
    unnamed x15, local copies, waits for them, and re-layouts  9.68 us
    dot_general x1, matrix products, per_device(): lax.dot_general(picked, weight, (((2,), (2,)), ((0,), (0,))), preferred_e...  7.73 us
    select_n x1, other arithmetic, unpack_counts(): packed_words % 65536  7.1 us
    all_to_all x1, starting transfers between devices, per_device(): lax.all_to_all(src_field, 'narrow', split_axis=2, concat_axis=1, tiled=True)  4.23 us
  transfers between devices with their start and end apart: 10, of which 3 were waited for; matrix products, arithmetic and copies ran while one was open for 9% of the time, Pallas kernels for 0%

commit v1 on v0

v1 whole, which is shorter than its diff:
```python
import functools

import jax
import jax.numpy as jnp
from jax import lax
from jax.experimental import pallas as pl
from jax.experimental.pallas import tpu as pltpu
from jax.sharding import PartitionSpec as P

DENOM = 256
TB_DEV = 64
REGIONS = 5

wet_limit = 0.001


def round_up(value, multiple):
    return -(-value // multiple) * multiple


def sum_kernel(
    source_ref, slot_ref, base_ref, packed_ref, *rest, groups, part_levels, rows, in_kernel
):
    if in_kernel:
        pieces = rest[:groups]
        depth_ref = rest[groups]
        rest = rest[groups + 1 :]
        outs = rest[: 4 * groups]
        acc_ref, stack_ref = rest[4 * groups :]
    else:
        stack_ref = rest[0]
        outs = rest[1 : 1 + 4 * groups]
        acc_ref = rest[1 + 4 * groups]
    step = pl.program_id(0)
    per_step = packed_ref.shape[0]

    @pl.when(step == 0)
    def _():
        acc_ref[...] = jnp.zeros_like(acc_ref)
        if in_kernel:
            tiles = stack_ref.shape[0]
            for tile in range(tiles):
                cut = pl.ds(tile * 128, 128)
                depth = depth_ref[:, cut]
                parts = []
                for k in range(groups):
                    level = base_ref[k] + lax.broadcasted_iota(jnp.int32, (part_levels, 128), 0)
                    wet = level < depth
                    for v in range(pieces[k].shape[0]):
                        cells = pieces[k][v, :, cut].astype(jnp.float32)
                        parts.append(jnp.where(wet, cells, 0.0))
                    parts.append(jnp.where(wet, 1.0, 0.0))
                stack_ref[tile] = jnp.concatenate(parts, axis=0).astype(jnp.bfloat16)

    for q in range(per_step):
        pair = step * per_step + q
        words = packed_ref[q]
        low = (words & 65535).astype(jnp.float32)
        high = (words >> 16).astype(jnp.float32)
        weight = (jnp.concatenate([low, high], axis=0) * (1.0 / DENOM)).astype(jnp.bfloat16)
        term = lax.dot_general(
            stack_ref[source_ref[pair]],
            weight,
            (((1,), (1,)), ((), ())),
            preferred_element_type=jnp.float32,
        )
        acc_ref[slot_ref[pair]] += term

    @pl.when(step == pl.num_programs(0) - 1)
    def _():
        for k in range(groups):
            cut = slice(k * rows, (k + 1) * rows)
            for o, (first, last) in enumerate(((0, 2), (2, 3), (3, 4), (4, 5))):
                value = acc_ref[first * TB_DEV : last * TB_DEV, cut, :]
                out = outs[4 * k + o]
                out[...] = value.reshape(out.shape).astype(out.dtype)


def pair_sums(source, slot, base, packed, cells, groups, part_levels, rows, in_kernel):
    slots, half, block = packed.shape
    per_step = 16 if slots % 16 == 0 else 1
    whole = lambda a: pl.BlockSpec(a.shape, lambda i, *_: (0,) * a.ndim)
    regions = (2, 1, 1, 1)
    shapes = [
        jax.ShapeDtypeStruct((r * TB_DEV * rows, block), jnp.bfloat16)
        for _ in range(groups)
        for r in regions
    ]
    scratch = [pltpu.VMEM((REGIONS * TB_DEV + 1, groups * rows, block), jnp.float32)]
    if in_kernel:
        tiles = cells[-1].shape[1] // block
        scratch.append(pltpu.VMEM((tiles, groups * rows, block), jnp.bfloat16))
    return pl.pallas_call(
        functools.partial(
            sum_kernel, groups=groups, part_levels=part_levels, rows=rows, in_kernel=in_kernel
        ),
        out_shape=shapes,
        grid_spec=pltpu.PrefetchScalarGridSpec(
            num_scalar_prefetch=3,
            grid=(slots // per_step,),
            in_specs=[pl.BlockSpec((per_step, half, block), lambda i, *_: (i, 0, 0))]
            + [whole(c) for c in cells],
            out_specs=[whole(s) for s in shapes],
            scratch_shapes=scratch,
        ),
        compiler_params=pltpu.CompilerParams(dimension_semantics=("arbitrary",)),
        name="pair_sums",
    )(source, slot, base, packed, *cells)


def divide_kernel(*refs, part_levels, field_vars):
    out_ref = refs[-1]
    rows = (field_vars + 1) * part_levels

    for b in range(TB_DEV):
        cut = slice(b * rows, (b + 1) * rows)
        total = refs[0][cut, :].astype(jnp.float32)
        for ref in refs[1:-1]:
            total = total + ref[cut, :].astype(jnp.float32)
        wet = total[field_vars * part_levels :]
        covered = wet > wet_limit
        safe = jnp.where(covered, wet, 1.0)
        for v in range(field_vars):
            value = total[v * part_levels : (v + 1) * part_levels] / safe
            out_ref[v, :, b * 128 : (b + 1) * 128] = jnp.where(covered, value, 0.0).astype(
                out_ref.dtype
            )


def divided(parts, part_levels, field_vars, rows, in_kernel):
    block = parts[0].shape[1]
    shape = (field_vars, part_levels, TB_DEV * block)
    if in_kernel:
        return pl.pallas_call(
            functools.partial(divide_kernel, part_levels=part_levels, field_vars=field_vars),
            out_shape=jax.ShapeDtypeStruct(shape, jnp.bfloat16),
            name="divide",
        )(*parts)
    total = sum(p.astype(jnp.float32) for p in parts).reshape(TB_DEV, rows, block)
    total = total[:, : (field_vars + 1) * part_levels].reshape(TB_DEV, -1, part_levels, block)
    wet = total[:, field_vars:]
    covered = wet > wet_limit
    value = total[:, :field_vars] / jnp.where(covered, wet, 1.0)
    value = jnp.where(covered, value, 0.0)
    return jnp.transpose(value, (1, 2, 0, 3)).reshape(shape).astype(jnp.bfloat16)


def per_device(src_field, src_depth, packed_counts, pair_source, pair_home, pair_count):
    groups = lax.axis_size("narrow")
    wide_size = lax.axis_size("wide")
    field_vars, part_levels, _ = src_field.shape
    block = packed_counts.shape[2]
    own_cells = src_depth.shape[0]
    tiles = own_cells // block
    pair_slots = pair_source.shape[0]
    rows = round_up((field_vars + 1) * part_levels, 8)
    in_kernel = part_levels % 8 == 0 and block == 128
    narrow_index = lax.axis_index("narrow")
    wide_index = lax.axis_index("wide")

    pieces = []
    for k in range(groups):
        start = ((narrow_index + k) % groups) * own_cells
        piece = lax.dynamic_slice_in_dim(src_field, start, own_cells, 2)
        if k:
            piece = lax.ppermute(piece, "narrow", [(i, (i + k) % groups) for i in range(groups)])
        pieces.append(piece)
    steps = jnp.arange(groups, dtype=jnp.int32)
    base = ((narrow_index - steps + groups) % groups * part_levels).astype(jnp.int32)

    chips = wide_size // 2
    core, chip = wide_index % 2, wide_index // 2
    side = chip % 2
    target = pair_home // TB_DEV
    step = (target // 2 - chip + 1 + chips) % chips - 1
    across = jnp.where(side == 0, 1, -1)
    same_core = target % 2 == core
    region = jnp.where(
        same_core,
        jnp.where(step == 0, 4, jnp.where(step == across, 3, 2)),
        jnp.where(step == 0, 0, 1),
    )
    live = jnp.arange(pair_slots, dtype=jnp.int32) < pair_count[0]
    slot = jnp.where(live, region * TB_DEV + pair_home % TB_DEV, REGIONS * TB_DEV)
    slot = slot.astype(jnp.int32)

    if in_kernel:
        cells = pieces + [src_depth.reshape(1, own_cells)]
    else:
        stack = []
        for k in range(groups):
            level = base[k] + jnp.arange(part_levels, dtype=jnp.int32)
            wet = level[:, None] < src_depth[None, :]
            masked = jnp.where(wet[None], pieces[k], jnp.zeros_like(pieces[k]))
            both = jnp.concatenate([masked, wet[None].astype(jnp.bfloat16)], axis=0)
            both = both.reshape(-1, own_cells)
            stack.append(jnp.pad(both, ((0, rows - both.shape[0]), (0, 0))))
        stack = jnp.concatenate(stack, axis=0).reshape(groups * rows, tiles, block)
        cells = [jnp.transpose(stack, (1, 0, 2))]
    sums = pair_sums(
        pair_source, slot, base, packed_counts, cells, groups, part_levels, rows, in_kernel
    )

    to_core = [(w, w ^ 1) for w in range(wide_size)]
    to_column = [(w, (w + (4 if w // 2 % 2 else -4)) % wide_size) for w in range(wide_size)]
    to_side = [(w, w ^ 2) for w in range(wide_size)]
    for_column = core != side
    unit = TB_DEV * rows
    zero = jnp.zeros((), jnp.float32)
    wider = lambda a: a.astype(jnp.float32)
    final = []
    for k in list(range(1, groups)) + [0]:
        out_core, own_column, own_side, own_home = sums[4 * k : 4 * k + 4]
        from_core = lax.ppermute(out_core, "wide", to_core)
        partner_home, partner_away = from_core[:unit], wider(from_core[unit:])
        column = wider(own_column) + jnp.where(for_column, partner_away, zero)
        from_column = lax.ppermute(column.astype(jnp.bfloat16), "wide", to_column)
        side_sum = wider(own_side) + jnp.where(for_column, zero, partner_away)
        side_sum = side_sum + wider(from_column)
        from_side = lax.ppermute(side_sum.astype(jnp.bfloat16), "wide", to_side)
        if k:
            total = wider(own_home) + wider(partner_home) + wider(from_side)
            route = [(i, (i - k) % groups) for i in range(groups)]
            final.append(lax.ppermute(total.astype(jnp.bfloat16), "narrow", route))
        else:
            final += [own_home, partner_home, from_side]
    return divided(final, part_levels, field_vars, rows, in_kernel)


def solution(mesh):
    placed = (
        P(None, "narrow", "wide"),
        P(("wide", "narrow")),
        P(("wide", "narrow"), None, None),
        P(("wide", "narrow")),
        P(("wide", "narrow")),
        P(("wide", "narrow")),
    )
    return jax.shard_map(
        per_device, mesh=mesh, in_specs=placed, out_specs=P(None, "narrow", "wide"), check_vma=False
    )
```

time: 142 us -> 59.1 us (0.42)
  waiting for transfers between devices: 54.6 us -> 22 us
  local copies, waits for them, and re-layouts: 30.3 us -> 3.68 us
  between operations: 14.4 us -> 0.7 us
  Pallas kernels: 0 us -> 12.6 us
  matrix products: 11.5 us -> 0 us
  other arithmetic: 11.4 us -> 5.47 us
  starting transfers between devices: 19.5 us -> 14.2 us
    reduce_scatter x1 -> x0, waiting for transfers between devices: 25.3 us -> none  [per_device(): lax.psum_scatter(partial_value, 'narrow', scatter_dimension=0, tiled=True)]
    scatter x2 -> x0, local copies, waits for them, and re-layouts: 12.7 us -> none  [the longest x1 11.7 us: per_device(): outgoing = jnp.zeros((offset_count * capacity, levels * components, block...]
    pallas_call x0 -> x2, Pallas kernels: none -> 12.6 us  [the longest x1 10.3 us: pair_sums(): pl.pallas_call(functools.partial(sum_kernel, groups=groups, part_levels=p...]
    dot_general x6 -> x0, matrix products: 11.5 us -> none  [the longest x1 7.73 us: per_device(): lax.dot_general(picked, weight, (((2,), (2,)), ((0,), (0,))), preferred_e...]
    unnamed x15 -> x10, local copies, waits for them, and re-layouts: 9.68 us -> 1.39 us
    ppermute x8, waiting for transfers between devices: 29.3 us -> 22 us  [the longest x2 12 us: per_device(): from_column = lax.ppermute(column.astype(jnp.bfloat16), 'wide', to_column)]
    select_n x4 -> x1, other arithmetic: 7.13 us -> 1.19 us  [per_device(): jnp.where(live, region * TB_DEV + pair_home % TB_DEV, REGIONS * TB_DEV)]
    all_to_all x1 -> x0, starting transfers between devices: 4.23 us -> none  [per_device(): lax.all_to_all(src_field, 'narrow', split_axis=2, concat_axis=1, tiled=True)]
  transfers between devices with their start and end apart: 10 -> 8, of which waited for: 3 -> 6; matrix products, arithmetic and copies ran while one was open for 9% -> 11% of each run, Pallas kernels for 0% -> 0%
where the time goes in v1:
time: 59.1 us; the launch traced here: 58.7 us
  waiting for transfers between devices  22 us (37%)
  starting transfers between devices  14.2 us (24%)
  Pallas kernels  12.6 us (21%)
  other arithmetic  5.47 us (9%)
  local copies, waits for them, and re-layouts  3.68 us (6%)
  between operations  0.7 us (1%)
    ppermute x2, waiting for transfers between devices, per_device(): from_column = lax.ppermute(column.astype(jnp.bfloat16), 'wide', to_column)  12 us
    pallas_call x1, Pallas kernels, pair_sums(): pl.pallas_call(functools.partial(sum_kernel, groups=groups, part_levels=p...  10.3 us
    ppermute x2, waiting for transfers between devices, per_device(): from_side = lax.ppermute(side_sum.astype(jnp.bfloat16), 'wide', to_side)  7.13 us
    ppermute x2, starting transfers between devices, per_device(): from_side = lax.ppermute(side_sum.astype(jnp.bfloat16), 'wide', to_side)  4.59 us
    ppermute x2, starting transfers between devices, per_device(): from_column = lax.ppermute(column.astype(jnp.bfloat16), 'wide', to_column)  4.57 us
    ppermute x1, starting transfers between devices, per_device(): lax.ppermute(piece, 'narrow', [(i, (i + k) % groups) for i in range(group...  2.97 us
    pallas_call x1, Pallas kernels, divided(): pl.pallas_call(functools.partial(divide_kernel, part_levels=part_levels,...  2.31 us
    convert_element_type x2, other arithmetic, per_device(): from_column = lax.ppermute(column.astype(jnp.bfloat16), 'wide', to_column)  2.25 us
  transfers between devices with their start and end apart: 8, of which 6 were waited for; matrix products, arithmetic and copies ran while one was open for 11% of the time, Pallas kernels for 0%

profile of v1, /device:TPU:0, one launch (start us, length us, event | category | flops | bytes accessed | tf_op | source)
XLA Modules:
  0.0 58.7 jit_solution(11278977156850345618)
XLA Ops:
  0.0 1.5 %constant_dynamic-slice_fusion = (bf16[2,8,2048]{2,1,0:T(8,128)(2,1)S(1)}, bf16[2,8,2048]{2,1,0:T(8,128)(2,1)}) fusion(bf16[2,8,4096]{2,1,0:T(8,128)(2,1)} %param.6, s32[]{:T(128)S(6)} %select_n.120, s32[]{:T(128)S(6)} %select_n.118), kind=kLoop, calls=%fused_computation.41 | loop fusion | bytes 262152 | tf_op jit(solution)/shard_map/dynamic_slice | solution.py:164
  1.5 3.0 %collective-permute-start = (bf16[2,8,2048]{2,1,0:T(8,128)(2,1)S(1)}, bf16[2,8,2048]{2,1,0:T(8,128)(2,1)S(1)}, u32[]{:S(2)}, u32[]{:S(2)}) collective-permute-start(bf16[2,8,2048]{2,1,0:T(8,128)(2,1)S(1)} %get-tuple-element.21), channel_id=1, source_target_pairs={{0,1},{1,0},{2,3},{3,2},{4,5},{5,4},{6,7},{7,6},{8,9},{9,8},{10,11... | collective-permute-start | bytes 196616 | tf_op jit(solution)/shard_map/ppermute | solution.py:166
  5.1 1.2 %compare_select_fusion.6.slot_ref = s32[128]{0:T(128)} fusion(s32[128]{0:T(128)} %param.10, s32[]{:T(128)S(6)} %select_n.109, s32[]{:T(128)S(6)} %select_n.106, s32[]{:T(128)S(6)} %select_n.104, s32[]{:T(128)} %bitcast.2), kind=kLoop, calls=%fused_computation.27 | loop fusion | flops 8064 | bytes 1040 | tf_op jit(solution)/shard_map/jit(_where)/select_n | solution.py:184
  6.3 0.5 fusion.12.base_ref
  6.8 0.0 collective-permute-done.rest_1_
  6.8 0.0 copy-start.4
  6.8 0.6 %copy-done.4 = bf16[2,8,2048]{2,1,0:T(8,128)(2,1)} copy-done((bf16[2,8,2048]{2,1,0:T(8,128)(2,1)}, bf16[2,8,2048]{2,1,0:T(8,128)(2,1)S(1)}, u32[]{:S(2)}) %copy-start.4) | copy-done | bytes 65560
  7.5 10.3 %pair_sums.1 = (bf16[3072,128]{1,0:T(8,128)(2,1)}, bf16[1536,128]{1,0:T(8,128)(2,1)}, bf16[1536,128]{1,0:T(8,128)(2,1)}, bf16[1536,128]{1,0:T(8,128)(2,1)}, bf16...) custom-call(s32[128]{0:T(128)} %source_ref.1, ...), custom_call_target="tpu_custom_call" | custom-call | tf_op jit(solution)/shard_map/pair_sums/pallas_call | solution.py:93
  17.8 0.0 copy-start.3
  17.8 0.0 copy-start.2
  17.8 0.1 collective-permute-start.1
  17.9 0.5 collective-permute-start.5
  18.4 2.0 %collective-permute-done.1 = bf16[3072,128]{1,0:T(8,128)(2,1)S(1)} collective-permute-done((bf16[3072,128]{1,0:T(8,128)(2,1)}, bf16[3072,128]{1,0:T(8,128)(2,1)S(1)}, u32[]{:S(2)}, u32[]{:S(2)}) %collective-permute-start.1) | collective-permute-done | bytes 786464 | tf_op jit(solution)/shard_map/ppermute | solution.py:214
  20.4 1.1 %fusion.4 = bf16[1536,128]{1,0:T(8,128)(2,1)S(1)} fusion(bf16[1536,128]{1,0:T(8,128)(2,1)} %get-tuple-element.16, pred[]{:T(512)S(6)} %ne.83, bf16[3072,128]{1,0:T(8,128)(2,1)S(1)} %collective-permute-done.1), kind=kLoop, calls=%fused_computation.8 | loop fusion | flops 983040 | bytes 1179649 | tf_op jit(solution)/shard_map/convert_element_type | solution.py:217
  21.5 4.1 %collective-permute-start.2 = (bf16[1536,128]{1,0:T(8,128)(2,1)S(1)}, bf16[1536,128]{1,0:T(8,128)(2,1)S(1)}, u32[]{:S(2)}, u32[]{:S(2)}) collective-permute-start(bf16[1536,128]{1,0:T(8,128)(2,1)S(1)} %fusion.4), channel_id=1, source_target_pairs={{0,24},{2,26},{4,12},{6,14},{8,0},{10,2},{12,20},{14,22},{16,8},{1... | collective-permute-start | bytes 1179656 | tf_op jit(solution)/shard_map/ppermute | solution.py:217
  25.6 0.0 collective-permute-done.5
  25.6 1.1 %fusion.9 = bf16[1536,128]{1,0:T(8,128)(2,1)S(1)} fusion(bf16[1536,128]{1,0:T(8,128)(2,1)} %get-tuple-element.20, pred[]{:T(512)S(6)} %ne.83, bf16[3072,128]{1,0:T(8,128)(2,1)S(1)} %collective-permute-done.5), kind=kLoop, calls=%fused_computation.13 | loop fusion | flops 983040 | bytes 1179649 | tf_op jit(solution)/shard_map/convert_element_type | solution.py:217
  26.7 0.5 collective-permute-start.6
  27.2 7.9 %collective-permute-done.2 = bf16[1536,128]{1,0:T(8,128)(2,1)S(1)} collective-permute-done((bf16[1536,128]{1,0:T(8,128)(2,1)S(1)}, bf16[1536,128]{1,0:T(8,128)(2,1)S(1)}, u32[]{:S(2)}, u32[]{:S(2)}) %collective-permute-start.2) | collective-permute-done | bytes 393248 | tf_op jit(solution)/shard_map/ppermute | solution.py:217
  35.1 1.2 %fusion.2 = bf16[1536,128]{1,0:T(8,128)(2,1)S(1)} fusion(bf16[1536,128]{1,0:T(8,128)(2,1)S(1)} %collective-permute-done.2, bf16[1536,128]{1,0:T(8,128)(2,1)} %get-tuple-element.15, pred[]{:T(512)S(6)} %ne.83, bf16[3072,128]{1,0:T(8,128)(2,1)S(1)} %collective-permute-done.1), kind=kLoop, calls=%fused_computation.6 | loop fusion | flops 1376256 | bytes 1572865 | tf_op jit(solution)/shard_map/convert_element_type | solution.py:220
  36.3 2.3 %collective-permute-start.3 = (bf16[1536,128]{1,0:T(8,128)(2,1)S(1)}, bf16[1536,128]{1,0:T(8,128)(2,1)S(1)}, u32[]{:S(2)}, u32[]{:S(2)}) collective-permute-start(bf16[1536,128]{1,0:T(8,128)(2,1)S(1)} %fusion.2), channel_id=1, source_target_pairs={{0,4},{2,6},{4,0},{6,2},{8,12},{10,14},{12,8},{14,10},{16,20},{18,... | collective-permute-start | bytes 1179656 | tf_op jit(solution)/shard_map/ppermute | solution.py:220
  38.5 4.2 %collective-permute-done.6 = bf16[1536,128]{1,0:T(8,128)(2,1)S(1)} collective-permute-done((bf16[1536,128]{1,0:T(8,128)(2,1)S(1)}, bf16[1536,128]{1,0:T(8,128)(2,1)S(1)}, u32[]{:S(2)}, u32[]{:S(2)}) %collective-permute-start.6) | collective-permute-done | bytes 393248 | tf_op jit(solution)/shard_map/ppermute | solution.py:217
  42.7 0.0 copy-done.3
  42.7 0.2 fusion.7
  42.9 2.3 %collective-permute-start.7 = (bf16[1536,128]{1,0:T(8,128)(2,1)S(1)}, bf16[1536,128]{1,0:T(8,128)(2,1)S(1)}, u32[]{:S(2)}, u32[]{:S(2)}) collective-permute-start(bf16[1536,128]{1,0:T(8,128)(2,1)S(1)} %fusion.7), channel_id=1, source_target_pairs={{0,4},{2,6},{4,0},{6,2},{8,12},{10,14},{12,8},{14,10},{16,20},{18,... | collective-permute-start | bytes 1179656 | tf_op jit(solution)/shard_map/ppermute | solution.py:220
  45.2 2.2 %collective-permute-done.3 = bf16[1536,128]{1,0:T(8,128)(2,1)S(1)} collective-permute-done((bf16[1536,128]{1,0:T(8,128)(2,1)S(1)}, bf16[1536,128]{1,0:T(8,128)(2,1)S(1)}, u32[]{:S(2)}, u32[]{:S(2)}) %collective-permute-start.3) | collective-permute-done | bytes 393248 | tf_op jit(solution)/shard_map/ppermute | solution.py:220
  47.4 0.0 copy-done.2
  47.4 0.2 add_convert_fusion
  47.6 1.5 %collective-permute-start.4 = (bf16[1536,128]{1,0:T(8,128)(2,1)S(1)}, bf16[1536,128]{1,0:T(8,128)(2,1)S(1)}, u32[]{:S(2)}, u32[]{:S(2)}) collective-permute-start(bf16[1536,128]{1,0:T(8,128)(2,1)S(1)} %add_convert_fusion), channel_id=1, source_target_pairs={{0,1},{1,0},{2,3},{3,2},{4,5},{5,4},{6,7},{7,6},{8,9},{9,8},{10,11... | collective-permute-start | bytes 1179656 | tf_op jit(solution)/shard_map/ppermute | solution.py:224
  49.1 0.8 %slice.18.refs_2_ = bf16[1536,128]{1,0:T(8,128)(2,1)} slice(bf16[3072,128]{1,0:T(8,128)(2,1)S(1)} %collective-permute-done.5), slice={[0:1536], [0:128]} | slice | bytes 786432 | tf_op jit(solution)/shard_map/slice | solution.py:215
  49.9 4.9 %collective-permute-done.7.refs_3_ = bf16[1536,128]{1,0:T(8,128)(2,1)S(1)} collective-permute-done((bf16[1536,128]{1,0:T(8,128)(2,1)S(1)}, bf16[1536,128]{1,0:T(8,128)(2,1)S(1)}, u32[]{:S(2)}, u32[]{:S(2)}) %collective-permute-start.7) | collective-permute-done | bytes 393248 | tf_op jit(solution)/shard_map/ppermute | solution.py:220
  54.8 0.0 copy-start
  54.8 0.8 %collective-permute-done.4.refs_0_ = bf16[1536,128]{1,0:T(8,128)(2,1)S(1)} collective-permute-done((bf16[1536,128]{1,0:T(8,128)(2,1)S(1)}, bf16[1536,128]{1,0:T(8,128)(2,1)S(1)}, u32[]{:S(2)}, u32[]{:S(2)}) %collective-permute-start.4) | collective-permute-done | bytes 393248 | tf_op jit(solution)/shard_map/ppermute | solution.py:224
  55.7 0.0 copy-start.1
  55.7 0.0 copy-done
  55.7 0.7 %copy-done.1 = bf16[1536,128]{1,0:T(8,128)(2,1)} copy-done((bf16[1536,128]{1,0:T(8,128)(2,1)}, bf16[1536,128]{1,0:T(8,128)(2,1)S(1)}, u32[]{:S(2)}) %copy-start.1) | copy-done | bytes 393240
  56.4 2.3 %divide.1 = bf16[2,8,8192]{2,1,0:T(8,128)(2,1)} custom-call(bf16[1536,128]{1,0:T(8,128)(2,1)} %copy-done.1, bf16[1536,128]{1,0:T(8,128)(2,1)} %get-tuple-element.17.refs_1_, bf16[1536,128]{1,0:T(8,128)(2,1)} %slice.18.refs_2_, bf16[1536,128]{1,0:T(8,128)(2,1)} %copy-done), custom_call_target="tpu_custom_call" | custom-call | tf_op jit(solution)/shard_map/divide/pallas_call | solution.py:134
Async XLA Ops:
  1.5 5.3 %collective-permute-start = (bf16[2,8,2048]{2,1,0:T(8,128)(2,1)S(1)}, bf16[2,8,2048]{2,1,0:T(8,128)(2,1)S(1)}, u32[]{:S(2)}, u32[]{:S(2)}) collective-permute-start(bf16[2,8,2048]{2,1,0:T(8,128)(2,1)S(1)} %get-tuple-element.21), channel_id=1, source_target_pairs={{0,1},{1,0},{2,3},{3,2},{4,5},{5,4},{6,7},{7,6},{8,9},{9,8},{10,11... | collective-permute-start | bytes 196616 | tf_op jit(solution)/shard_map/ppermute | solution.py:166
  6.8 0.6 %copy-start.4 = (bf16[2,8,2048]{2,1,0:T(8,128)(2,1)}, bf16[2,8,2048]{2,1,0:T(8,128)(2,1)S(1)}, u32[]{:S(2)}) copy-start(bf16[2,8,2048]{2,1,0:T(8,128)(2,1)S(1)} %collective-permute-done.rest_1_) | copy-start | bytes 196612
  17.8 24.9 %copy-start.3 = (bf16[1536,128]{1,0:T(8,128)(2,1)S(1)}, bf16[1536,128]{1,0:T(8,128)(2,1)}, u32[]{:S(2)}) copy-start(bf16[1536,128]{1,0:T(8,128)(2,1)} %get-tuple-element.19) | copy-start | bytes 1179652
  17.8 29.6 %copy-start.2 = (bf16[1536,128]{1,0:T(8,128)(2,1)S(1)}, bf16[1536,128]{1,0:T(8,128)(2,1)}, u32[]{:S(2)}) copy-start(bf16[1536,128]{1,0:T(8,128)(2,1)} %get-tuple-element.13) | copy-start | bytes 1179652
  17.8 2.6 %collective-permute-start.1 = (bf16[3072,128]{1,0:T(8,128)(2,1)}, bf16[3072,128]{1,0:T(8,128)(2,1)S(1)}, u32[]{:S(2)}, u32[]{:S(2)}) collective-permute-start(bf16[3072,128]{1,0:T(8,128)(2,1)} %get-tuple-element.14), channel_id=1, source_target_pairs={{0,2},{2,0},{4,6},{6,4},{8,10},{10,8},{12,14},{14,12},{16,18},{18,... | collective-permute-start | bytes 2359304 | tf_op jit(solution)/shard_map/ppermute | solution.py:214
  17.9 7.7 %collective-permute-start.5 = (bf16[3072,128]{1,0:T(8,128)(2,1)}, bf16[3072,128]{1,0:T(8,128)(2,1)S(1)}, u32[]{:S(2)}, u32[]{:S(2)}) collective-permute-start(bf16[3072,128]{1,0:T(8,128)(2,1)} %get-tuple-element.18), channel_id=1, source_target_pairs={{0,2},{2,0},{4,6},{6,4},{8,10},{10,8},{12,14},{14,12},{16,18},{18,... | collective-permute-start | bytes 2359304 | tf_op jit(solution)/shard_map/ppermute | solution.py:214
  21.5 13.6 %collective-permute-start.2 = (bf16[1536,128]{1,0:T(8,128)(2,1)S(1)}, bf16[1536,128]{1,0:T(8,128)(2,1)S(1)}, u32[]{:S(2)}, u32[]{:S(2)}) collective-permute-start(bf16[1536,128]{1,0:T(8,128)(2,1)S(1)} %fusion.4), channel_id=1, source_target_pairs={{0,24},{2,26},{4,12},{6,14},{8,0},{10,2},{12,20},{14,22},{16,8},{1... | collective-permute-start | bytes 1179656 | tf_op jit(solution)/shard_map/ppermute | solution.py:217
  26.7 16.0 %collective-permute-start.6 = (bf16[1536,128]{1,0:T(8,128)(2,1)S(1)}, bf16[1536,128]{1,0:T(8,128)(2,1)S(1)}, u32[]{:S(2)}, u32[]{:S(2)}) collective-permute-start(bf16[1536,128]{1,0:T(8,128)(2,1)S(1)} %fusion.9), channel_id=1, source_target_pairs={{0,24},{2,26},{4,12},{6,14},{8,0},{10,2},{12,20},{14,22},{16,8},{1... | collective-permute-start | bytes 1179656 | tf_op jit(solution)/shard_map/ppermute | solution.py:217
  36.3 11.1 %collective-permute-start.3 = (bf16[1536,128]{1,0:T(8,128)(2,1)S(1)}, bf16[1536,128]{1,0:T(8,128)(2,1)S(1)}, u32[]{:S(2)}, u32[]{:S(2)}) collective-permute-start(bf16[1536,128]{1,0:T(8,128)(2,1)S(1)} %fusion.2), channel_id=1, source_target_pairs={{0,4},{2,6},{4,0},{6,2},{8,12},{10,14},{12,8},{14,10},{16,20},{18,... | collective-permute-start | bytes 1179656 | tf_op jit(solution)/shard_map/ppermute | solution.py:220
  42.9 12.0 %collective-permute-start.7 = (bf16[1536,128]{1,0:T(8,128)(2,1)S(1)}, bf16[1536,128]{1,0:T(8,128)(2,1)S(1)}, u32[]{:S(2)}, u32[]{:S(2)}) collective-permute-start(bf16[1536,128]{1,0:T(8,128)(2,1)S(1)} %fusion.7), channel_id=1, source_target_pairs={{0,4},{2,6},{4,0},{6,2},{8,12},{10,14},{12,8},{14,10},{16,20},{18,... | collective-permute-start | bytes 1179656 | tf_op jit(solution)/shard_map/ppermute | solution.py:220
  47.6 8.1 %collective-permute-start.4 = (bf16[1536,128]{1,0:T(8,128)(2,1)S(1)}, bf16[1536,128]{1,0:T(8,128)(2,1)S(1)}, u32[]{:S(2)}, u32[]{:S(2)}) collective-permute-start(bf16[1536,128]{1,0:T(8,128)(2,1)S(1)} %add_convert_fusion), channel_id=1, source_target_pairs={{0,1},{1,0},{2,3},{3,2},{4,5},{5,4},{6,7},{7,6},{8,9},{9,8},{10,11... | collective-permute-start | bytes 1179656 | tf_op jit(solution)/shard_map/ppermute | solution.py:224
  54.8 0.8 %copy-start = (bf16[1536,128]{1,0:T(8,128)(2,1)}, bf16[1536,128]{1,0:T(8,128)(2,1)S(1)}, u32[]{:S(2)}) copy-start(bf16[1536,128]{1,0:T(8,128)(2,1)S(1)} %collective-permute-done.7.refs_3_) | copy-start | bytes 1179652
  55.7 0.7 %copy-start.1 = (bf16[1536,128]{1,0:T(8,128)(2,1)}, bf16[1536,128]{1,0:T(8,128)(2,1)S(1)}, u32[]{:S(2)}) copy-start(bf16[1536,128]{1,0:T(8,128)(2,1)S(1)} %collective-permute-done.4.refs_0_) | copy-start | bytes 1179652

commit v2 on v1

--- a/solution.py
+++ b/solution.py
@@ -10,6 +10,7 @@
 DENOM = 256
 TB_DEV = 64
 REGIONS = 5
+FIRST_PART = 36
 
 wet_limit = 0.001
 
@@ -114,8 +115,9 @@
 
     for b in range(TB_DEV):
         cut = slice(b * rows, (b + 1) * rows)
-        total = refs[0][cut, :].astype(jnp.float32)
-        for ref in refs[1:-1]:
+        part, place = (0, b) if b < FIRST_PART else (1, b - FIRST_PART)
+        total = refs[part][place * rows : (place + 1) * rows, :].astype(jnp.float32)
+        for ref in refs[2:-1]:
             total = total + ref[cut, :].astype(jnp.float32)
         wet = total[field_vars * part_levels :]
         covered = wet > wet_limit
@@ -127,15 +129,17 @@
             )
 
 
-def divided(parts, part_levels, field_vars, rows, in_kernel):
+def divided(parts, halves, part_levels, field_vars, rows, in_kernel):
     block = parts[0].shape[1]
+    unit = TB_DEV * rows
     shape = (field_vars, part_levels, TB_DEV * block)
     if in_kernel:
         return pl.pallas_call(
             functools.partial(divide_kernel, part_levels=part_levels, field_vars=field_vars),
             out_shape=jax.ShapeDtypeStruct(shape, jnp.bfloat16),
             name="divide",
-        )(*parts)
+        )(*halves, *parts)
+    parts = [p[:unit] for p in parts] + [jnp.concatenate(halves, axis=0)]
     total = sum(p.astype(jnp.float32) for p in parts).reshape(TB_DEV, rows, block)
     total = total[:, : (field_vars + 1) * part_levels].reshape(TB_DEV, -1, part_levels, block)
     wet = total[:, field_vars:]
@@ -208,23 +212,44 @@
     unit = TB_DEV * rows
     zero = jnp.zeros((), jnp.float32)
     wider = lambda a: a.astype(jnp.float32)
-    final = []
-    for k in list(range(1, groups)) + [0]:
-        out_core, own_column, own_side, own_home = sums[4 * k : 4 * k + 4]
-        from_core = lax.ppermute(out_core, "wide", to_core)
-        partner_home, partner_away = from_core[:unit], wider(from_core[unit:])
-        column = wider(own_column) + jnp.where(for_column, partner_away, zero)
-        from_column = lax.ppermute(column.astype(jnp.bfloat16), "wide", to_column)
-        side_sum = wider(own_side) + jnp.where(for_column, zero, partner_away)
-        side_sum = side_sum + wider(from_column)
-        from_side = lax.ppermute(side_sum.astype(jnp.bfloat16), "wide", to_side)
-        if k:
-            total = wider(own_home) + wider(partner_home) + wider(from_side)
-            route = [(i, (i - k) % groups) for i in range(groups)]
-            final.append(lax.ppermute(total.astype(jnp.bfloat16), "narrow", route))
-        else:
-            final += [own_home, partner_home, from_side]
-    return divided(final, part_levels, field_vars, rows, in_kernel)
+    narrower = lambda a: a.astype(jnp.bfloat16)
+    back = [[(i, (i - k) % groups) for i in range(groups)] for k in range(groups)]
+    first = FIRST_PART * rows
+    halves = [slice(0, first), slice(first, unit)]
+    from_core = [lax.ppermute(sums[4 * k], "wide", to_core) for k in range(groups)]
+
+    def column_part(k, half):
+        away = wider(from_core[k][unit:][half])
+        return wider(sums[4 * k + 1][half]) + jnp.where(for_column, away, zero)
+
+    def side_part(k, half):
+        away = wider(from_core[k][unit:][half])
+        return wider(sums[4 * k + 2][half]) + jnp.where(for_column, zero, away)
+
+    column_sent = [
+        [lax.ppermute(narrower(column_part(k, half)), "narrow", back[k]) for k in range(1, groups)]
+        for half in halves
+    ]
+    other_side = [
+        lax.ppermute(narrower(side_part(k, slice(0, unit))), "wide", to_side)
+        for k in range(1, groups)
+    ]
+    from_column = []
+    for half, received in zip(halves, column_sent):
+        column = column_part(0, half)
+        for piece in received:
+            column = column + wider(piece)
+        from_column.append(lax.ppermute(narrower(column), "wide", to_column))
+    from_narrow = []
+    for k in range(1, groups):
+        total = wider(sums[4 * k + 3]) + wider(from_core[k][:unit]) + wider(other_side[k - 1])
+        from_narrow.append(lax.ppermute(narrower(total), "narrow", back[k]))
+    from_side = [
+        lax.ppermute(narrower(side_part(0, half) + wider(piece)), "wide", to_side)
+        for half, piece in zip(halves, from_column)
+    ]
+    final = [sums[3], from_core[0]] + from_narrow
+    return divided(final, from_side, part_levels, field_vars, rows, in_kernel)
 
 
 def solution(mesh):

time: 59.1 us -> 55.9 us (0.946)
  waiting for transfers between devices: 22 us -> 13.1 us
  starting transfers between devices: 14.2 us -> 18.5 us
  other arithmetic: 5.47 us -> 7.27 us
  local copies, waits for them, and re-layouts: 3.68 us -> 2.99 us
    ppermute x7 -> x10, waiting for transfers between devices: 22 us -> 13.1 us  [the longest x2 7.6 us: per_device(): lax.ppermute(narrower(side_part(0, half) + wider(piece)), 'wide', to_side)]
    ppermute x7 -> x10, starting transfers between devices: 11.3 us -> 15.5 us  [the longest x2 6.91 us: per_device(): from_column.append(lax.ppermute(narrower(column), 'wide', to_column))]
    convert_element_type x5 -> x8, other arithmetic: 3.77 us -> 5.51 us  [per_device(): narrower = lambda a: a.astype(jnp.bfloat16)]
    slice x1 -> x0, local copies, waits for them, and re-layouts: 0.79 us -> none  [per_device(): partner_home, partner_away = (from_core[:unit], wider(from_core[unit:]))]
    unnamed x10 -> x14, local copies, waits for them, and re-layouts: 1.39 us -> 1.48 us
  transfers between devices with their start and end apart: 8 -> 11, of which waited for: 6 -> 4; matrix products, arithmetic and copies ran while one was open for 11% -> 13% of each run, Pallas kernels for 0% -> 0%
where the time goes in v2:
time: 55.9 us; the launch traced here: 55.4 us
  starting transfers between devices  18.5 us (33%)
  waiting for transfers between devices  13.1 us (23%)
  Pallas kernels  12.8 us (23%)
  other arithmetic  7.27 us (13%)
  local copies, waits for them, and re-layouts  2.99 us (5%)
  between operations  0.73 us (1%)
    pallas_call x1, Pallas kernels, pair_sums(): pl.pallas_call(functools.partial(sum_kernel, groups=groups, part_levels=p...  10.4 us
    ppermute x2, waiting for transfers between devices, per_device(): lax.ppermute(narrower(side_part(0, half) + wider(piece)), 'wide', to_side)  7.6 us
    ppermute x2, starting transfers between devices, per_device(): from_column.append(lax.ppermute(narrower(column), 'wide', to_column))  6.91 us
    convert_element_type x8, other arithmetic, per_device(): narrower = lambda a: a.astype(jnp.bfloat16)  5.51 us
    ppermute x1, starting transfers between devices, per_device(): lax.ppermute(piece, 'narrow', [(i, (i + k) % groups) for i in range(group...  2.97 us
    pallas_call x1, Pallas kernels, divided(): pl.pallas_call(functools.partial(divide_kernel, part_levels=part_levels,...  2.47 us
    ppermute x2, starting transfers between devices, per_device(): lax.ppermute(narrower(side_part(0, half) + wider(piece)), 'wide', to_side)  2.42 us
    ppermute x2, waiting for transfers between devices, per_device(): from_column.append(lax.ppermute(narrower(column), 'wide', to_column))  2.41 us
  transfers between devices with their start and end apart: 11, of which 4 were waited for; matrix products, arithmetic and copies ran while one was open for 13% of the time, Pallas kernels for 0%

profile of v2, /device:TPU:0, one launch (start us, length us, event | category | flops | bytes accessed | tf_op | source)
XLA Modules:
  0.0 55.4 jit_solution(9204830057382235485)
XLA Ops:
  0.0 1.5 %constant_dynamic-slice_fusion = (bf16[2,8,2048]{2,1,0:T(8,128)(2,1)S(1)}, bf16[2,8,2048]{2,1,0:T(8,128)(2,1)}) fusion(bf16[2,8,4096]{2,1,0:T(8,128)(2,1)} %param.6, s32[]{:T(128)S(6)} %select_n.142, s32[]{:T(128)S(6)} %select_n.140), kind=kLoop, calls=%fused_computation.46 | loop fusion | bytes 262152 | tf_op jit(solution)/shard_map/dynamic_slice | solution.py:168
  1.5 3.0 %collective-permute-start = (bf16[2,8,2048]{2,1,0:T(8,128)(2,1)S(1)}, bf16[2,8,2048]{2,1,0:T(8,128)(2,1)S(1)}, u32[]{:S(2)}, u32[]{:S(2)}) collective-permute-start(bf16[2,8,2048]{2,1,0:T(8,128)(2,1)S(1)} %get-tuple-element.21), channel_id=1, source_target_pairs={{0,1},{1,0},{2,3},{3,2},{4,5},{5,4},{6,7},{7,6},{8,9},{9,8},{10,11... | collective-permute-start | bytes 196616 | tf_op jit(solution)/shard_map/ppermute | solution.py:170
  5.1 1.2 %compare_select_fusion.6.slot_ref = s32[128]{0:T(128)} fusion(s32[128]{0:T(128)} %param.10, s32[]{:T(128)S(6)} %select_n.131, s32[]{:T(128)S(6)} %select_n.128, s32[]{:T(128)S(6)} %select_n.126, s32[]{:T(128)} %bitcast.2), kind=kLoop, calls=%fused_computation.32 | loop fusion | flops 8064 | bytes 1040 | tf_op jit(solution)/shard_map/jit(_where)/select_n | solution.py:188
  6.4 0.5 fusion.14.base_ref
  6.9 0.0 collective-permute-done.rest_1_
  6.9 0.0 copy-start.6
  6.9 0.6 %copy-done.6 = bf16[2,8,2048]{2,1,0:T(8,128)(2,1)} copy-done((bf16[2,8,2048]{2,1,0:T(8,128)(2,1)}, bf16[2,8,2048]{2,1,0:T(8,128)(2,1)S(1)}, u32[]{:S(2)}) %copy-start.6) | copy-done | bytes 65560
  7.5 10.4 %pair_sums.1 = (bf16[3072,128]{1,0:T(8,128)(2,1)}, bf16[1536,128]{1,0:T(8,128)(2,1)}, bf16[1536,128]{1,0:T(8,128)(2,1)}, bf16[1536,128]{1,0:T(8,128)(2,1)}, bf16...) custom-call(s32[128]{0:T(128)} %source_ref.1, ...), custom_call_target="tpu_custom_call" | custom-call | tf_op jit(solution)/shard_map/pair_sums/pallas_call | solution.py:94
  17.9 0.0 copy-start.2
  17.9 0.0 copy-start.1
  17.9 0.1 collective-permute-start.2
  18.0 0.5 collective-permute-start.1
  18.5 2.0 %collective-permute-done.2 = bf16[3072,128]{1,0:T(8,128)(2,1)S(1)} collective-permute-done((bf16[3072,128]{1,0:T(8,128)(2,1)}, bf16[3072,128]{1,0:T(8,128)(2,1)S(1)}, u32[]{:S(2)}, u32[]{:S(2)}) %collective-permute-start.2) | collective-permute-done | bytes 786464 | tf_op jit(solution)/shard_map/ppermute | solution.py:219
  20.4 1.0 %add_convert_fusion.3 = bf16[672,128]{1,0:T(8,128)(2,1)S(1)} fusion(bf16[3072,128]{1,0:T(8,128)(2,1)S(1)} %collective-permute-done.2, bf16[1536,128]{1,0:T(8,128)(2,1)} %get-tuple-element.16, pred[]{:T(512)S(6)} %ne.83), kind=kLoop, calls=%fused_computation.19 | loop fusion | flops 430080 | bytes 516097 | tf_op jit(solution)/shard_map/convert_element_type | solution.py:215
  21.4 1.9 %collective-permute-start.6 = (bf16[672,128]{1,0:T(8,128)(2,1)S(1)}, bf16[672,128]{1,0:T(8,128)(2,1)S(1)}, u32[]{:S(2)}, u32[]{:S(2)}) collective-permute-start(bf16[672,128]{1,0:T(8,128)(2,1)S(1)} %add_convert_fusion.3), channel_id=1, source_target_pairs={{0,1},{1,0},{2,3},{3,2},{4,5},{5,4},{6,7},{7,6},{8,9},{9,8},{10,11... | collective-permute-start | bytes 516104 | tf_op jit(solution)/shard_map/ppermute | solution.py:230
  23.3 1.0 %add_convert_fusion.2 = bf16[864,128]{1,0:T(8,128)(2,1)S(1)} fusion(bf16[3072,128]{1,0:T(8,128)(2,1)S(1)} %collective-permute-done.2, bf16[1536,128]{1,0:T(8,128)(2,1)} %get-tuple-element.16, pred[]{:T(512)S(6)} %ne.83), kind=kLoop, calls=%fused_computation.10 | loop fusion | flops 552960 | bytes 663553 | tf_op jit(solution)/shard_map/convert_element_type | solution.py:215
  24.3 0.2 collective-permute-start.3
  24.6 1.1 %add_convert_fusion.1 = bf16[1536,128]{1,0:T(8,128)(2,1)S(1)} fusion(bf16[1536,128]{1,0:T(8,128)(2,1)} %get-tuple-element.20, bf16[3072,128]{1,0:T(8,128)(2,1)S(1)} %collective-permute-done.2, pred[]{:T(512)S(6)} %ne.83), kind=kLoop, calls=%fused_computation.1 | loop fusion | flops 983040 | bytes 1179649 | tf_op jit(solution)/shard_map/convert_element_type | solution.py:215
  25.7 1.9 %collective-permute-start.9 = (bf16[1536,128]{1,0:T(8,128)(2,1)S(1)}, bf16[1536,128]{1,0:T(8,128)(2,1)S(1)}, u32[]{:S(2)}, u32[]{:S(2)}) collective-permute-start(bf16[1536,128]{1,0:T(8,128)(2,1)S(1)} %add_convert_fusion.1), channel_id=1, source_target_pairs={{0,4},{2,6},{4,0},{6,2},{8,12},{10,14},{12,8},{14,10},{16,20},{18,... | collective-permute-start | bytes 1179656 | tf_op jit(solution)/shard_map/ppermute | solution.py:234
  27.6 0.0 collective-permute-done.1.refs_3_
  27.6 0.0 copy-start
  27.6 1.1 %collective-permute-done.6 = bf16[672,128]{1,0:T(8,128)(2,1)S(1)} collective-permute-done((bf16[672,128]{1,0:T(8,128)(2,1)S(1)}, bf16[672,128]{1,0:T(8,128)(2,1)S(1)}, u32[]{:S(2)}, u32[]{:S(2)}) %collective-permute-start.6) | collective-permute-done | bytes 172064 | tf_op jit(solution)/shard_map/ppermute | solution.py:230
  28.7 1.0 %fusion.11 = bf16[672,128]{1,0:T(8,128)(2,1)S(1)} fusion(bf16[672,128]{1,0:T(8,128)(2,1)S(1)} %collective-permute-done.6, bf16[1536,128]{1,0:T(8,128)(2,1)} %get-tuple-element.15, pred[]{:T(512)S(6)} %ne.83, bf16[3072,128]{1,0:T(8,128)(2,1)S(1)} %collective-permute-done.1.refs_3_), kind=kLoop, calls=%fused_computation.18 | loop fusion | flops 602112 | bytes 688129 | tf_op jit(solution)/shard_map/convert_element_type | solution.py:215
  29.7 4.0 %collective-permute-start.7 = (bf16[672,128]{1,0:T(8,128)(2,1)S(1)}, bf16[672,128]{1,0:T(8,128)(2,1)S(1)}, u32[]{:S(2)}, u32[]{:S(2)}) collective-permute-start(bf16[672,128]{1,0:T(8,128)(2,1)S(1)} %fusion.11), channel_id=1, source_target_pairs={{0,24},{2,26},{4,12},{6,14},{8,0},{10,2},{12,20},{14,22},{16,8},{1... | collective-permute-start | bytes 516104 | tf_op jit(solution)/shard_map/ppermute | solution.py:242
  33.7 0.0 collective-permute-done.3
  33.7 1.0 %fusion.5 = bf16[864,128]{1,0:T(8,128)(2,1)S(1)} fusion(bf16[864,128]{1,0:T(8,128)(2,1)S(1)} %collective-permute-done.3, bf16[1536,128]{1,0:T(8,128)(2,1)} %get-tuple-element.15, pred[]{:T(512)S(6)} %ne.83, bf16[3072,128]{1,0:T(8,128)(2,1)S(1)} %collective-permute-done.1.refs_3_), kind=kLoop, calls=%fused_computation.9 | loop fusion | flops 774144 | bytes 884737 | tf_op jit(solution)/shard_map/convert_element_type | solution.py:215
  34.8 2.9 %collective-permute-start.4 = (bf16[864,128]{1,0:T(8,128)(2,1)S(1)}, bf16[864,128]{1,0:T(8,128)(2,1)S(1)}, u32[]{:S(2)}, u32[]{:S(2)}) collective-permute-start(bf16[864,128]{1,0:T(8,128)(2,1)S(1)} %fusion.5), channel_id=1, source_target_pairs={{0,24},{2,26},{4,12},{6,14},{8,0},{10,2},{12,20},{14,22},{16,8},{1... | collective-permute-start | bytes 663560 | tf_op jit(solution)/shard_map/ppermute | solution.py:242
  37.7 0.0 collective-permute-done.9
  37.7 0.0 copy-done.2
  37.7 0.2 add_convert_fusion
  37.9 1.6 %collective-permute-start.10 = (bf16[1536,128]{1,0:T(8,128)(2,1)S(1)}, bf16[1536,128]{1,0:T(8,128)(2,1)S(1)}, u32[]{:S(2)}, u32[]{:S(2)}) collective-permute-start(bf16[1536,128]{1,0:T(8,128)(2,1)S(1)} %add_convert_fusion), channel_id=1, source_target_pairs={{0,1},{1,0},{2,3},{3,2},{4,5},{5,4},{6,7},{7,6},{8,9},{9,8},{10,11... | collective-permute-start | bytes 1179656 | tf_op jit(solution)/shard_map/ppermute | solution.py:246
  39.4 2.4 %collective-permute-done.4 = bf16[864,128]{1,0:T(8,128)(2,1)S(1)} collective-permute-done((bf16[864,128]{1,0:T(8,128)(2,1)S(1)}, bf16[864,128]{1,0:T(8,128)(2,1)S(1)}, u32[]{:S(2)}, u32[]{:S(2)}) %collective-permute-start.4) | collective-permute-done | bytes 221216 | tf_op jit(solution)/shard_map/ppermute | solution.py:242
  41.8 0.0 copy-done.1
  41.8 0.1 fusion.2
  41.9 2.3 %collective-permute-start.5 = (bf16[864,128]{1,0:T(8,128)(2,1)S(1)}, bf16[864,128]{1,0:T(8,128)(2,1)S(1)}, u32[]{:S(2)}, u32[]{:S(2)}) collective-permute-start(bf16[864,128]{1,0:T(8,128)(2,1)S(1)} %fusion.2), channel_id=1, source_target_pairs={{0,4},{2,6},{4,0},{6,2},{8,12},{10,14},{12,8},{14,10},{16,20},{18,... | collective-permute-start | bytes 663560 | tf_op jit(solution)/shard_map/ppermute | solution.py:248
  44.3 0.0 collective-permute-done.7
  44.3 0.1 fusion.8
  44.4 0.1 collective-permute-start.8
  44.5 7.6 %collective-permute-done.8.refs_1_ = bf16[672,128]{1,0:T(8,128)(2,1)S(1)} collective-permute-done((bf16[672,128]{1,0:T(8,128)(2,1)S(1)}, bf16[672,128]{1,0:T(8,128)(2,1)S(1)}, u32[]{:S(2)}, u32[]{:S(2)}) %collective-permute-start.8) | collective-permute-done | bytes 172064 | tf_op jit(solution)/shard_map/ppermute | solution.py:248
  52.1 0.0 copy-start.5
  52.1 0.0 collective-permute-done.5.refs_0_
  52.1 0.0 collective-permute-done.10.refs_4_
  52.1 0.0 copy-start.3
  52.1 0.0 copy-done
  52.1 0.6 %copy-done.5 = bf16[672,128]{1,0:T(8,128)(2,1)} copy-done((bf16[672,128]{1,0:T(8,128)(2,1)}, bf16[672,128]{1,0:T(8,128)(2,1)S(1)}, u32[]{:S(2)}) %copy-start.5) | copy-done | bytes 172056
  52.7 0.1 copy-done.4
  52.8 0.1 copy-done.3
  52.9 2.5 %divide.1 = bf16[2,8,8192]{2,1,0:T(8,128)(2,1)} custom-call(bf16[864,128]{1,0:T(8,128)(2,1)} %copy-done.4, bf16[672,128]{1,0:T(8,128)(2,1)} %copy-done.5, bf16[1536,128]{1,0:T(8,128)(2,1)} %get-tuple-element.18.refs_2_, bf16[3072,128]{1,0:T(8,128)(2,1)} %copy-done, bf16[1536,128]{1,0:T(8,128)(2,1)} %copy-done.3), custom_call_target="tpu_custom_call" | custom-call | tf_op jit(solution)/shard_map/divide/pallas_call | solution.py:137
  (1 shorter events, 0.0 us)
Async XLA Ops:
  1.5 5.4 %collective-permute-start = (bf16[2,8,2048]{2,1,0:T(8,128)(2,1)S(1)}, bf16[2,8,2048]{2,1,0:T(8,128)(2,1)S(1)}, u32[]{:S(2)}, u32[]{:S(2)}) collective-permute-start(bf16[2,8,2048]{2,1,0:T(8,128)(2,1)S(1)} %get-tuple-element.21), channel_id=1, source_target_pairs={{0,1},{1,0},{2,3},{3,2},{4,5},{5,4},{6,7},{7,6},{8,9},{9,8},{10,11... | collective-permute-start | bytes 196616 | tf_op jit(solution)/shard_map/ppermute | solution.py:170
  6.9 0.6 %copy-start.6 = (bf16[2,8,2048]{2,1,0:T(8,128)(2,1)}, bf16[2,8,2048]{2,1,0:T(8,128)(2,1)S(1)}, u32[]{:S(2)}) copy-start(bf16[2,8,2048]{2,1,0:T(8,128)(2,1)S(1)} %collective-permute-done.rest_1_) | copy-start | bytes 196612
  17.9 19.8 %copy-start.2 = (bf16[1536,128]{1,0:T(8,128)(2,1)S(1)}, bf16[1536,128]{1,0:T(8,128)(2,1)}, u32[]{:S(2)}) copy-start(bf16[1536,128]{1,0:T(8,128)(2,1)} %get-tuple-element.19) | copy-start | bytes 1179652
  17.9 24.0 %copy-start.1 = (bf16[1536,128]{1,0:T(8,128)(2,1)S(1)}, bf16[1536,128]{1,0:T(8,128)(2,1)}, u32[]{:S(2)}) copy-start(bf16[1536,128]{1,0:T(8,128)(2,1)} %get-tuple-element.13) | copy-start | bytes 1179652
  17.9 2.6 %collective-permute-start.2 = (bf16[3072,128]{1,0:T(8,128)(2,1)}, bf16[3072,128]{1,0:T(8,128)(2,1)S(1)}, u32[]{:S(2)}, u32[]{:S(2)}) collective-permute-start(bf16[3072,128]{1,0:T(8,128)(2,1)} %get-tuple-element.17), channel_id=1, source_target_pairs={{0,2},{2,0},{4,6},{6,4},{8,10},{10,8},{12,14},{14,12},{16,18},{18,... | collective-permute-start | bytes 2359304 | tf_op jit(solution)/shard_map/ppermute | solution.py:219
  18.0 9.7 %collective-permute-start.1 = (bf16[3072,128]{1,0:T(8,128)(2,1)}, bf16[3072,128]{1,0:T(8,128)(2,1)S(1)}, u32[]{:S(2)}, u32[]{:S(2)}) collective-permute-start(bf16[3072,128]{1,0:T(8,128)(2,1)} %get-tuple-element.14), channel_id=1, source_target_pairs={{0,2},{2,0},{4,6},{6,4},{8,10},{10,8},{12,14},{14,12},{16,18},{18,... | collective-permute-start | bytes 2359304 | tf_op jit(solution)/shard_map/ppermute | solution.py:219
  21.4 7.3 %collective-permute-start.6 = (bf16[672,128]{1,0:T(8,128)(2,1)S(1)}, bf16[672,128]{1,0:T(8,128)(2,1)S(1)}, u32[]{:S(2)}, u32[]{:S(2)}) collective-permute-start(bf16[672,128]{1,0:T(8,128)(2,1)S(1)} %add_convert_fusion.3), channel_id=1, source_target_pairs={{0,1},{1,0},{2,3},{3,2},{4,5},{5,4},{6,7},{7,6},{8,9},{9,8},{10,11... | collective-permute-start | bytes 516104 | tf_op jit(solution)/shard_map/ppermute | solution.py:230
  24.3 9.4 %collective-permute-start.3 = (bf16[864,128]{1,0:T(8,128)(2,1)S(1)}, bf16[864,128]{1,0:T(8,128)(2,1)S(1)}, u32[]{:S(2)}, u32[]{:S(2)}) collective-permute-start(bf16[864,128]{1,0:T(8,128)(2,1)S(1)} %add_convert_fusion.2), channel_id=1, source_target_pairs={{0,1},{1,0},{2,3},{3,2},{4,5},{5,4},{6,7},{7,6},{8,9},{9,8},{10,11... | collective-permute-start | bytes 663560 | tf_op jit(solution)/shard_map/ppermute | solution.py:230
  25.7 12.0 %collective-permute-start.9 = (bf16[1536,128]{1,0:T(8,128)(2,1)S(1)}, bf16[1536,128]{1,0:T(8,128)(2,1)S(1)}, u32[]{:S(2)}, u32[]{:S(2)}) collective-permute-start(bf16[1536,128]{1,0:T(8,128)(2,1)S(1)} %add_convert_fusion.1), channel_id=1, source_target_pairs={{0,4},{2,6},{4,0},{6,2},{8,12},{10,14},{12,8},{14,10},{16,20},{18,... | collective-permute-start | bytes 1179656 | tf_op jit(solution)/shard_map/ppermute | solution.py:234
  27.6 24.4 %copy-start = (bf16[3072,128]{1,0:T(8,128)(2,1)}, bf16[3072,128]{1,0:T(8,128)(2,1)S(1)}, u32[]{:S(2)}) copy-start(bf16[3072,128]{1,0:T(8,128)(2,1)S(1)} %collective-permute-done.1.refs_3_) | copy-start | bytes 2359300
  29.7 14.5 %collective-permute-start.7 = (bf16[672,128]{1,0:T(8,128)(2,1)S(1)}, bf16[672,128]{1,0:T(8,128)(2,1)S(1)}, u32[]{:S(2)}, u32[]{:S(2)}) collective-permute-start(bf16[672,128]{1,0:T(8,128)(2,1)S(1)} %fusion.11), channel_id=1, source_target_pairs={{0,24},{2,26},{4,12},{6,14},{8,0},{10,2},{12,20},{14,22},{16,8},{1... | collective-permute-start | bytes 516104 | tf_op jit(solution)/shard_map/ppermute | solution.py:242
  34.8 7.0 %collective-permute-start.4 = (bf16[864,128]{1,0:T(8,128)(2,1)S(1)}, bf16[864,128]{1,0:T(8,128)(2,1)S(1)}, u32[]{:S(2)}, u32[]{:S(2)}) collective-permute-start(bf16[864,128]{1,0:T(8,128)(2,1)S(1)} %fusion.5), channel_id=1, source_target_pairs={{0,24},{2,26},{4,12},{6,14},{8,0},{10,2},{12,20},{14,22},{16,8},{1... | collective-permute-start | bytes 663560 | tf_op jit(solution)/shard_map/ppermute | solution.py:242
  37.9 14.2 %collective-permute-start.10 = (bf16[1536,128]{1,0:T(8,128)(2,1)S(1)}, bf16[1536,128]{1,0:T(8,128)(2,1)S(1)}, u32[]{:S(2)}, u32[]{:S(2)}) collective-permute-start(bf16[1536,128]{1,0:T(8,128)(2,1)S(1)} %add_convert_fusion), channel_id=1, source_target_pairs={{0,1},{1,0},{2,3},{3,2},{4,5},{5,4},{6,7},{7,6},{8,9},{9,8},{10,11... | collective-permute-start | bytes 1179656 | tf_op jit(solution)/shard_map/ppermute | solution.py:246
  41.9 10.1 %collective-permute-start.5 = (bf16[864,128]{1,0:T(8,128)(2,1)S(1)}, bf16[864,128]{1,0:T(8,128)(2,1)S(1)}, u32[]{:S(2)}, u32[]{:S(2)}) collective-permute-start(bf16[864,128]{1,0:T(8,128)(2,1)S(1)} %fusion.2), channel_id=1, source_target_pairs={{0,4},{2,6},{4,0},{6,2},{8,12},{10,14},{12,8},{14,10},{16,20},{18,... | collective-permute-start | bytes 663560 | tf_op jit(solution)/shard_map/ppermute | solution.py:248
  44.4 7.7 %collective-permute-start.8 = (bf16[672,128]{1,0:T(8,128)(2,1)S(1)}, bf16[672,128]{1,0:T(8,128)(2,1)S(1)}, u32[]{:S(2)}, u32[]{:S(2)}) collective-permute-start(bf16[672,128]{1,0:T(8,128)(2,1)S(1)} %fusion.8), channel_id=1, source_target_pairs={{0,4},{2,6},{4,0},{6,2},{8,12},{10,14},{12,8},{14,10},{16,20},{18,... | collective-permute-start | bytes 516104 | tf_op jit(solution)/shard_map/ppermute | solution.py:248
  52.1 0.7 %copy-start.5 = (bf16[672,128]{1,0:T(8,128)(2,1)}, bf16[672,128]{1,0:T(8,128)(2,1)S(1)}, u32[]{:S(2)}) copy-start(bf16[672,128]{1,0:T(8,128)(2,1)S(1)} %collective-permute-done.8.refs_1_) | copy-start | bytes 516100
  52.1 0.7 %copy-start.4 = (bf16[864,128]{1,0:T(8,128)(2,1)}, bf16[864,128]{1,0:T(8,128)(2,1)S(1)}, u32[]{:S(2)}) copy-start(bf16[864,128]{1,0:T(8,128)(2,1)S(1)} %collective-permute-done.5.refs_0_) | copy-start | bytes 663556
  52.1 0.9 %copy-start.3 = (bf16[1536,128]{1,0:T(8,128)(2,1)}, bf16[1536,128]{1,0:T(8,128)(2,1)S(1)}, u32[]{:S(2)}) copy-start(bf16[1536,128]{1,0:T(8,128)(2,1)S(1)} %collective-permute-done.10.refs_4_) | copy-start | bytes 1179652

commit v3 on v2

--- a/solution.py
+++ b/solution.py
@@ -83,7 +83,7 @@
     whole = lambda a: pl.BlockSpec(a.shape, lambda i, *_: (0,) * a.ndim)
     regions = (2, 1, 1, 1)
     shapes = [
-        jax.ShapeDtypeStruct((r * TB_DEV * rows, block), jnp.bfloat16)
+        pltpu.VMEM((r * TB_DEV * rows, block), jnp.bfloat16)
         for _ in range(groups)
         for r in regions
     ]
@@ -101,10 +101,10 @@
             grid=(slots // per_step,),
             in_specs=[pl.BlockSpec((per_step, half, block), lambda i, *_: (i, 0, 0))]
             + [whole(c) for c in cells],
-            out_specs=[whole(s) for s in shapes],
+            out_specs=[pl.BlockSpec(memory_space=pltpu.VMEM)] * len(shapes),
             scratch_shapes=scratch,
         ),
-        compiler_params=pltpu.CompilerParams(dimension_semantics=("arbitrary",)),
+        compiler_params=pltpu.CompilerParams(dimension_semantics=("arbitrary",), vmem_limit_bytes=28 << 20),
         name="pair_sums",
     )(source, slot, base, packed, *cells)
 

time: 55.9 us -> 54 us (0.966)
  Pallas kernels: 12.8 us -> 8.82 us
  local copies, waits for them, and re-layouts: 2.99 us -> 6.03 us
  other arithmetic: 7.27 us -> 5.35 us
  starting transfers between devices: 18.5 us -> 19.8 us
    pallas_call x1, Pallas kernels: 10.4 us -> 6.34 us  [pair_sums(): pl.pallas_call(functools.partial(sum_kernel, groups=groups, part_levels=p...]
    unnamed x14 -> x16, local copies, waits for them, and re-layouts: 1.48 us -> 5.15 us
    ppermute x2, starting transfers between devices: 6.91 us -> 8 us  [per_device(): from_column.append(lax.ppermute(narrower(column), 'wide', to_column))]
    ppermute x2, waiting for transfers between devices: 2.41 us -> 1.42 us  [per_device(): from_column.append(lax.ppermute(narrower(column), 'wide', to_column))]
    ppermute x1, waiting for transfers between devices: 0.01 us -> 0.89 us  [per_device(): lax.ppermute(piece, 'narrow', [(i, (i + k) % groups) for i in range(group...]
    convert_element_type x8, other arithmetic: 5.51 us -> 4.65 us  [per_device(): narrower = lambda a: a.astype(jnp.bfloat16)]
    dynamic_slice x1, local copies, waits for them, and re-layouts: 1.51 us -> 0.88 us  [per_device(): piece = lax.dynamic_slice_in_dim(src_field, start, own_cells, 2)]
  transfers between devices with their start and end apart: 11 -> 11, of which waited for: 4 -> 5; matrix products, arithmetic and copies ran while one was open for 13% -> 10% of each run, Pallas kernels for 0% -> 0%
where the time goes in v3:
time: 54 us; the launch traced here: 53.6 us
  starting transfers between devices  19.8 us (37%)
  waiting for transfers between devices  12.9 us (24%)
  Pallas kernels  8.82 us (16%)
  local copies, waits for them, and re-layouts  6.03 us (11%)
  other arithmetic  5.35 us (10%)
  between operations  0.72 us (1%)
    ppermute x2, starting transfers between devices, per_device(): from_column.append(lax.ppermute(narrower(column), 'wide', to_column))  8 us
    ppermute x2, waiting for transfers between devices, per_device(): lax.ppermute(narrower(side_part(0, half) + wider(piece)), 'wide', to_side)  7.57 us
    pallas_call x1, Pallas kernels, pair_sums(): pl.pallas_call(functools.partial(sum_kernel, groups=groups, part_levels=p...  6.34 us
    unnamed x16, local copies, waits for them, and re-layouts  5.15 us
    convert_element_type x8, other arithmetic, per_device(): narrower = lambda a: a.astype(jnp.bfloat16)  4.65 us
    ppermute x1, starting transfers between devices, per_device(): lax.ppermute(piece, 'narrow', [(i, (i + k) % groups) for i in range(group...  3.03 us
    pallas_call x1, Pallas kernels, divided(): pl.pallas_call(functools.partial(divide_kernel, part_levels=part_levels,...  2.47 us
    ppermute x2, starting transfers between devices, per_device(): lax.ppermute(narrower(side_part(0, half) + wider(piece)), 'wide', to_side)  2.43 us
  transfers between devices with their start and end apart: 11, of which 5 were waited for; matrix products, arithmetic and copies ran while one was open for 10% of the time, Pallas kernels for 0%

profile of v3, /device:TPU:0, one launch (start us, length us, event | category | flops | bytes accessed | tf_op | source)
XLA Modules:
  0.0 53.6 jit_solution(15811823431098804946)
XLA Ops:
  0.0 0.9 %constant_dynamic-slice_fusion = (bf16[2,8,2048]{2,1,0:T(8,128)(2,1)S(1)}, bf16[2,8,2048]{2,1,0:T(8,128)(2,1)S(1)}) fusion(bf16[2,8,4096]{2,1,0:T(8,128)(2,1)} %param.6, s32[]{:T(128)S(6)} %select_n.142, s32[]{:T(128)S(6)} %select_n.140), kind=kLoop, calls=%fused_computation.46 | loop fusion | bytes 262152 | tf_op jit(solution)/shard_map/dynamic_slice | solution.py:168
  0.9 3.0 %collective-permute-start = (bf16[2,8,2048]{2,1,0:T(8,128)(2,1)S(1)}, bf16[2,8,2048]{2,1,0:T(8,128)(2,1)S(1)}, u32[]{:S(2)}, u32[]{:S(2)}) collective-permute-start(bf16[2,8,2048]{2,1,0:T(8,128)(2,1)S(1)} %get-tuple-element.21), channel_id=1, source_target_pairs={{0,1},{1,0},{2,3},{3,2},{4,5},{5,4},{6,7},{7,6},{8,9},{9,8},{10,11... | collective-permute-start | bytes 196616 | tf_op jit(solution)/shard_map/ppermute | solution.py:170
  4.6 0.7 %compare_select_fusion.6.slot_ref = s32[128]{0:T(128)S(1)} fusion(s32[128]{0:T(128)} %param.10, s32[]{:T(128)S(6)} %select_n.131, s32[]{:T(128)S(6)} %select_n.128, s32[]{:T(128)S(6)} %select_n.126, s32[]{:T(128)} %bitcast.2), kind=kLoop, calls=%fused_computation.32 | loop fusion | flops 8064 | bytes 1040 | tf_op jit(solution)/shard_map/jit(_where)/select_n | solution.py:188
  5.3 0.9 %collective-permute-done.rest_1_ = bf16[2,8,2048]{2,1,0:T(8,128)(2,1)S(1)} collective-permute-done((bf16[2,8,2048]{2,1,0:T(8,128)(2,1)S(1)}, bf16[2,8,2048]{2,1,0:T(8,128)(2,1)S(1)}, u32[]{:S(2)}, u32[]{:S(2)}) %collective-permute-start) | collective-permute-done | bytes 65568 | tf_op jit(solution)/shard_map/ppermute | solution.py:170
  6.2 0.0 copy-start
  6.2 2.2 %copy-done = s32[128,64,128]{2,1,0:T(8,128)S(1)} copy-done((s32[128,64,128]{2,1,0:T(8,128)S(1)}, s32[128,64,128]{2,1,0:T(8,128)}, u32[]{:S(2)}) %copy-start) | copy-done | bytes 4194328
  8.4 0.0 copy-start.2
  8.4 0.7 %copy-done.2 = s32[2048]{0:T(1024)S(1)} copy-done((s32[2048]{0:T(1024)S(1)}, s32[2048]{0:T(1024)}, u32[]{:S(2)}) %copy-start.2) | copy-done | bytes 8216
  9.0 0.0 copy-start.3
  9.1 0.7 %copy-done.3 = s32[128]{0:T(128)S(1)} copy-done((s32[128]{0:T(128)S(1)}, s32[128]{0:T(128)}, u32[]{:S(2)}) %copy-start.3) | copy-done | bytes 536
  9.7 6.3 %pair_sums.1 = (bf16[3072,128]{1,0:T(8,128)(2,1)S(1)}, bf16[1536,128]{1,0:T(8,128)(2,1)S(1)}, bf16[1536,128]{1,0:T(8,128)(2,1)S(1)}, bf16[1536,128]{1,0:T(8,128)...) custom-call(s32[128]{0:T(128)S(1)} %copy-done.3, ...), custom_call_target="tpu_custom_call" | custom-call | tf_op jit(solution)/shard_map/pair_sums/pallas_call | solution.py:94
  16.0 0.0 copy-start.1
  16.1 0.8 %copy-done.1 = bf16[1536,128]{1,0:T(8,128)(2,1)} copy-done((bf16[1536,128]{1,0:T(8,128)(2,1)}, bf16[1536,128]{1,0:T(8,128)(2,1)S(1)}, u32[]{:S(2)}) %copy-start.1) | copy-done | bytes 393240
  16.8 0.0 collective-permute-start.2
  16.8 0.5 collective-permute-start.1
  17.3 2.1 %collective-permute-done.2 = bf16[3072,128]{1,0:T(8,128)(2,1)} collective-permute-done((bf16[3072,128]{1,0:T(8,128)(2,1)}, bf16[3072,128]{1,0:T(8,128)(2,1)}, u32[]{:S(2)}, u32[]{:S(2)}) %collective-permute-start.2) | collective-permute-done | bytes 786464 | tf_op jit(solution)/shard_map/ppermute | solution.py:219
  19.4 1.0 %add_convert_fusion.3 = bf16[672,128]{1,0:T(8,128)(2,1)S(1)} fusion(bf16[3072,128]{1,0:T(8,128)(2,1)} %collective-permute-done.2, bf16[1536,128]{1,0:T(8,128)(2,1)S(1)} %get-tuple-element.16, pred[]{:T(512)S(6)} %ne.83), kind=kLoop, calls=%fused_computation.19 | loop fusion | flops 430080 | bytes 516097 | tf_op jit(solution)/shard_map/convert_element_type | solution.py:215
  20.4 2.1 %collective-permute-start.6 = (bf16[672,128]{1,0:T(8,128)(2,1)S(1)}, bf16[672,128]{1,0:T(8,128)(2,1)S(1)}, u32[]{:S(2)}, u32[]{:S(2)}) collective-permute-start(bf16[672,128]{1,0:T(8,128)(2,1)S(1)} %add_convert_fusion.3), channel_id=1, source_target_pairs={{0,1},{1,0},{2,3},{3,2},{4,5},{5,4},{6,7},{7,6},{8,9},{9,8},{10,11... | collective-permute-start | bytes 516104 | tf_op jit(solution)/shard_map/ppermute | solution.py:230
  22.5 1.0 %add_convert_fusion.2 = bf16[864,128]{1,0:T(8,128)(2,1)S(1)} fusion(bf16[3072,128]{1,0:T(8,128)(2,1)} %collective-permute-done.2, bf16[1536,128]{1,0:T(8,128)(2,1)S(1)} %get-tuple-element.16, pred[]{:T(512)S(6)} %ne.83), kind=kLoop, calls=%fused_computation.10 | loop fusion | flops 552960 | bytes 663553 | tf_op jit(solution)/shard_map/convert_element_type | solution.py:215
  23.5 0.1 collective-permute-start.3
  23.6 1.1 %add_convert_fusion.1 = bf16[1536,128]{1,0:T(8,128)(2,1)S(1)} fusion(bf16[1536,128]{1,0:T(8,128)(2,1)S(1)} %get-tuple-element.20, bf16[3072,128]{1,0:T(8,128)(2,1)} %collective-permute-done.2, pred[]{:T(512)S(6)} %ne.83), kind=kLoop, calls=%fused_computation.1 | loop fusion | flops 983040 | bytes 1179649 | tf_op jit(solution)/shard_map/convert_element_type | solution.py:215
  24.7 2.1 %collective-permute-start.9 = (bf16[1536,128]{1,0:T(8,128)(2,1)S(1)}, bf16[1536,128]{1,0:T(8,128)(2,1)S(1)}, u32[]{:S(2)}, u32[]{:S(2)}) collective-permute-start(bf16[1536,128]{1,0:T(8,128)(2,1)S(1)} %add_convert_fusion.1), channel_id=1, source_target_pairs={{0,4},{2,6},{4,0},{6,2},{8,12},{10,14},{12,8},{14,10},{16,20},{18,... | collective-permute-start | bytes 1179656 | tf_op jit(solution)/shard_map/ppermute | solution.py:234
  26.8 0.0 collective-permute-done.1.refs_3_
  26.8 0.0 copy-start.4
  26.8 0.9 %collective-permute-done.6 = bf16[672,128]{1,0:T(8,128)(2,1)S(1)} collective-permute-done((bf16[672,128]{1,0:T(8,128)(2,1)S(1)}, bf16[672,128]{1,0:T(8,128)(2,1)S(1)}, u32[]{:S(2)}, u32[]{:S(2)}) %collective-permute-start.6) | collective-permute-done | bytes 172064 | tf_op jit(solution)/shard_map/ppermute | solution.py:230
  27.7 0.1 fusion.11
  27.8 4.2 %collective-permute-start.7 = (bf16[672,128]{1,0:T(8,128)(2,1)S(1)}, bf16[672,128]{1,0:T(8,128)(2,1)S(1)}, u32[]{:S(2)}, u32[]{:S(2)}) collective-permute-start(bf16[672,128]{1,0:T(8,128)(2,1)S(1)} %fusion.11), channel_id=1, source_target_pairs={{0,24},{2,26},{4,12},{6,14},{8,0},{10,2},{12,20},{14,22},{16,8},{1... | collective-permute-start | bytes 516104 | tf_op jit(solution)/shard_map/ppermute | solution.py:242
  32.0 0.0 collective-permute-done.3
  32.0 0.1 fusion.5
  32.1 3.8 %collective-permute-start.4 = (bf16[864,128]{1,0:T(8,128)(2,1)S(1)}, bf16[864,128]{1,0:T(8,128)(2,1)S(1)}, u32[]{:S(2)}, u32[]{:S(2)}) collective-permute-start(bf16[864,128]{1,0:T(8,128)(2,1)S(1)} %fusion.5), channel_id=1, source_target_pairs={{0,24},{2,26},{4,12},{6,14},{8,0},{10,2},{12,20},{14,22},{16,8},{1... | collective-permute-start | bytes 663560 | tf_op jit(solution)/shard_map/ppermute | solution.py:242
  35.9 0.0 collective-permute-done.9
  35.9 1.2 %add_convert_fusion = bf16[1536,128]{1,0:T(8,128)(2,1)S(1)} fusion(bf16[1536,128]{1,0:T(8,128)(2,1)S(1)} %collective-permute-done.9, bf16[1536,128]{1,0:T(8,128)(2,1)S(1)} %get-tuple-element.19, bf16[3072,128]{1,0:T(8,128)(2,1)} %collective-permute-done.2), kind=kLoop, calls=%fused_computation | loop fusion | flops 1179648 | bytes 1572864 | tf_op jit(solution)/shard_map/convert_element_type | solution.py:215
  37.1 1.6 %collective-permute-start.10 = (bf16[1536,128]{1,0:T(8,128)(2,1)S(1)}, bf16[1536,128]{1,0:T(8,128)(2,1)S(1)}, u32[]{:S(2)}, u32[]{:S(2)}) collective-permute-start(bf16[1536,128]{1,0:T(8,128)(2,1)S(1)} %add_convert_fusion), channel_id=1, source_target_pairs={{0,1},{1,0},{2,3},{3,2},{4,5},{5,4},{6,7},{7,6},{8,9},{9,8},{10,11... | collective-permute-start | bytes 1179656 | tf_op jit(solution)/shard_map/ppermute | solution.py:246
  38.6 1.4 %collective-permute-done.4 = bf16[864,128]{1,0:T(8,128)(2,1)S(1)} collective-permute-done((bf16[864,128]{1,0:T(8,128)(2,1)S(1)}, bf16[864,128]{1,0:T(8,128)(2,1)S(1)}, u32[]{:S(2)}, u32[]{:S(2)}) %collective-permute-start.4) | collective-permute-done | bytes 221216 | tf_op jit(solution)/shard_map/ppermute | solution.py:242
  40.1 0.1 fusion.2
  40.2 2.3 %collective-permute-start.5 = (bf16[864,128]{1,0:T(8,128)(2,1)S(1)}, bf16[864,128]{1,0:T(8,128)(2,1)S(1)}, u32[]{:S(2)}, u32[]{:S(2)}) collective-permute-start(bf16[864,128]{1,0:T(8,128)(2,1)S(1)} %fusion.2), channel_id=1, source_target_pairs={{0,4},{2,6},{4,0},{6,2},{8,12},{10,14},{12,8},{14,10},{16,20},{18,... | collective-permute-start | bytes 663560 | tf_op jit(solution)/shard_map/ppermute | solution.py:248
  42.5 0.0 collective-permute-done.7
  42.5 0.1 fusion.8
  42.6 0.0 copy-done.4
  42.6 0.1 collective-permute-start.8
  42.7 7.6 %collective-permute-done.8.refs_1_ = bf16[672,128]{1,0:T(8,128)(2,1)S(1)} collective-permute-done((bf16[672,128]{1,0:T(8,128)(2,1)S(1)}, bf16[672,128]{1,0:T(8,128)(2,1)S(1)}, u32[]{:S(2)}, u32[]{:S(2)}) %collective-permute-start.8) | collective-permute-done | bytes 172064 | tf_op jit(solution)/shard_map/ppermute | solution.py:248
  50.3 0.0 collective-permute-done.5.refs_0_
  50.3 0.0 collective-permute-done.10.refs_4_
  50.3 0.0 copy-start.5
  50.3 0.7 %copy-done.7 = bf16[672,128]{1,0:T(8,128)(2,1)} copy-done((bf16[672,128]{1,0:T(8,128)(2,1)}, bf16[672,128]{1,0:T(8,128)(2,1)S(1)}, u32[]{:S(2)}) %copy-start.7) | copy-done | bytes 172056
  51.0 0.1 copy-done.6
  51.0 0.1 copy-done.5
  51.1 2.5 %divide.1 = bf16[2,8,8192]{2,1,0:T(8,128)(2,1)} custom-call(bf16[864,128]{1,0:T(8,128)(2,1)} %copy-done.6, bf16[672,128]{1,0:T(8,128)(2,1)} %copy-done.7, bf16[1536,128]{1,0:T(8,128)(2,1)} %copy-done.1, bf16[3072,128]{1,0:T(8,128)(2,1)} %copy-done.4, bf16[1536,128]{1,0:T(8,128)(2,1)} %copy-done.5), custom_call_target="tpu_custom_call" | custom-call | tf_op jit(solution)/shard_map/divide/pallas_call | solution.py:137
  (3 shorter events, 0.0 us)
Async XLA Ops:
  0.9 5.3 %collective-permute-start = (bf16[2,8,2048]{2,1,0:T(8,128)(2,1)S(1)}, bf16[2,8,2048]{2,1,0:T(8,128)(2,1)S(1)}, u32[]{:S(2)}, u32[]{:S(2)}) collective-permute-start(bf16[2,8,2048]{2,1,0:T(8,128)(2,1)S(1)} %get-tuple-element.21), channel_id=1, source_target_pairs={{0,1},{1,0},{2,3},{3,2},{4,5},{5,4},{6,7},{7,6},{8,9},{9,8},{10,11... | collective-permute-start | bytes 196616 | tf_op jit(solution)/shard_map/ppermute | solution.py:170
  6.2 2.2 %copy-start = (s32[128,64,128]{2,1,0:T(8,128)S(1)}, s32[128,64,128]{2,1,0:T(8,128)}, u32[]{:S(2)}) copy-start(s32[128,64,128]{2,1,0:T(8,128)} %packed_ref.1) | copy-start | bytes 12582916
  8.4 0.7 %copy-start.2 = (s32[2048]{0:T(1024)S(1)}, s32[2048]{0:T(1024)}, u32[]{:S(2)}) copy-start(s32[2048]{0:T(1024)} %param.7) | copy-start | bytes 24580
  9.0 0.7 %copy-start.3 = (s32[128]{0:T(128)S(1)}, s32[128]{0:T(128)}, u32[]{:S(2)}) copy-start(s32[128]{0:T(128)} %source_ref.1) | copy-start | bytes 1540
  16.0 0.8 %copy-start.1 = (bf16[1536,128]{1,0:T(8,128)(2,1)}, bf16[1536,128]{1,0:T(8,128)(2,1)S(1)}, u32[]{:S(2)}) copy-start(bf16[1536,128]{1,0:T(8,128)(2,1)S(1)} %get-tuple-element.18.refs_2_) | copy-start | bytes 1179652
  16.8 2.6 %collective-permute-start.2 = (bf16[3072,128]{1,0:T(8,128)(2,1)}, bf16[3072,128]{1,0:T(8,128)(2,1)}, u32[]{:S(2)}, u32[]{:S(2)}) collective-permute-start(bf16[3072,128]{1,0:T(8,128)(2,1)} %get-tuple-element.17), channel_id=1, source_target_pairs={{0,2},{2,0},{4,6},{6,4},{8,10},{10,8},{12,14},{14,12},{16,18},{18,... | collective-permute-start | bytes 2359304 | tf_op jit(solution)/shard_map/ppermute | solution.py:219
  16.8 10.0 %collective-permute-start.1 = (bf16[3072,128]{1,0:T(8,128)(2,1)S(1)}, bf16[3072,128]{1,0:T(8,128)(2,1)S(1)}, u32[]{:S(2)}, u32[]{:S(2)}) collective-permute-start(bf16[3072,128]{1,0:T(8,128)(2,1)S(1)} %get-tuple-element.14), channel_id=1, source_target_pairs={{0,2},{2,0},{4,6},{6,4},{8,10},{10,8},{12,14},{14,12},{16,18},{18,... | collective-permute-start | bytes 2359304 | tf_op jit(solution)/shard_map/ppermute | solution.py:219
  20.4 7.3 %collective-permute-start.6 = (bf16[672,128]{1,0:T(8,128)(2,1)S(1)}, bf16[672,128]{1,0:T(8,128)(2,1)S(1)}, u32[]{:S(2)}, u32[]{:S(2)}) collective-permute-start(bf16[672,128]{1,0:T(8,128)(2,1)S(1)} %add_convert_fusion.3), channel_id=1, source_target_pairs={{0,1},{1,0},{2,3},{3,2},{4,5},{5,4},{6,7},{7,6},{8,9},{9,8},{10,11... | collective-permute-start | bytes 516104 | tf_op jit(solution)/shard_map/ppermute | solution.py:230
  23.5 8.5 %collective-permute-start.3 = (bf16[864,128]{1,0:T(8,128)(2,1)S(1)}, bf16[864,128]{1,0:T(8,128)(2,1)S(1)}, u32[]{:S(2)}, u32[]{:S(2)}) collective-permute-start(bf16[864,128]{1,0:T(8,128)(2,1)S(1)} %add_convert_fusion.2), channel_id=1, source_target_pairs={{0,1},{1,0},{2,3},{3,2},{4,5},{5,4},{6,7},{7,6},{8,9},{9,8},{10,11... | collective-permute-start | bytes 663560 | tf_op jit(solution)/shard_map/ppermute | solution.py:230
  24.7 11.2 %collective-permute-start.9 = (bf16[1536,128]{1,0:T(8,128)(2,1)S(1)}, bf16[1536,128]{1,0:T(8,128)(2,1)S(1)}, u32[]{:S(2)}, u32[]{:S(2)}) collective-permute-start(bf16[1536,128]{1,0:T(8,128)(2,1)S(1)} %add_convert_fusion.1), channel_id=1, source_target_pairs={{0,4},{2,6},{4,0},{6,2},{8,12},{10,14},{12,8},{14,10},{16,20},{18,... | collective-permute-start | bytes 1179656 | tf_op jit(solution)/shard_map/ppermute | solution.py:234
  26.8 15.8 %copy-start.4 = (bf16[3072,128]{1,0:T(8,128)(2,1)}, bf16[3072,128]{1,0:T(8,128)(2,1)S(1)}, u32[]{:S(2)}) copy-start(bf16[3072,128]{1,0:T(8,128)(2,1)S(1)} %collective-permute-done.1.refs_3_) | copy-start | bytes 2359300
  27.8 14.7 %collective-permute-start.7 = (bf16[672,128]{1,0:T(8,128)(2,1)S(1)}, bf16[672,128]{1,0:T(8,128)(2,1)S(1)}, u32[]{:S(2)}, u32[]{:S(2)}) collective-permute-start(bf16[672,128]{1,0:T(8,128)(2,1)S(1)} %fusion.11), channel_id=1, source_target_pairs={{0,24},{2,26},{4,12},{6,14},{8,0},{10,2},{12,20},{14,22},{16,8},{1... | collective-permute-start | bytes 516104 | tf_op jit(solution)/shard_map/ppermute | solution.py:242
  32.1 8.0 %collective-permute-start.4 = (bf16[864,128]{1,0:T(8,128)(2,1)S(1)}, bf16[864,128]{1,0:T(8,128)(2,1)S(1)}, u32[]{:S(2)}, u32[]{:S(2)}) collective-permute-start(bf16[864,128]{1,0:T(8,128)(2,1)S(1)} %fusion.5), channel_id=1, source_target_pairs={{0,24},{2,26},{4,12},{6,14},{8,0},{10,2},{12,20},{14,22},{16,8},{1... | collective-permute-start | bytes 663560 | tf_op jit(solution)/shard_map/ppermute | solution.py:242
  37.1 13.2 %collective-permute-start.10 = (bf16[1536,128]{1,0:T(8,128)(2,1)S(1)}, bf16[1536,128]{1,0:T(8,128)(2,1)S(1)}, u32[]{:S(2)}, u32[]{:S(2)}) collective-permute-start(bf16[1536,128]{1,0:T(8,128)(2,1)S(1)} %add_convert_fusion), channel_id=1, source_target_pairs={{0,1},{1,0},{2,3},{3,2},{4,5},{5,4},{6,7},{7,6},{8,9},{9,8},{10,11... | collective-permute-start | bytes 1179656 | tf_op jit(solution)/shard_map/ppermute | solution.py:246
  40.2 10.1 %collective-permute-start.5 = (bf16[864,128]{1,0:T(8,128)(2,1)S(1)}, bf16[864,128]{1,0:T(8,128)(2,1)S(1)}, u32[]{:S(2)}, u32[]{:S(2)}) collective-permute-start(bf16[864,128]{1,0:T(8,128)(2,1)S(1)} %fusion.2), channel_id=1, source_target_pairs={{0,4},{2,6},{4,0},{6,2},{8,12},{10,14},{12,8},{14,10},{16,20},{18,... | collective-permute-start | bytes 663560 | tf_op jit(solution)/shard_map/ppermute | solution.py:248
  42.6 7.7 %collective-permute-start.8 = (bf16[672,128]{1,0:T(8,128)(2,1)S(1)}, bf16[672,128]{1,0:T(8,128)(2,1)S(1)}, u32[]{:S(2)}, u32[]{:S(2)}) collective-permute-start(bf16[672,128]{1,0:T(8,128)(2,1)S(1)} %fusion.8), channel_id=1, source_target_pairs={{0,4},{2,6},{4,0},{6,2},{8,12},{10,14},{12,8},{14,10},{16,20},{18,... | collective-permute-start | bytes 516104 | tf_op jit(solution)/shard_map/ppermute | solution.py:248
  50.3 0.7 %copy-start.7 = (bf16[672,128]{1,0:T(8,128)(2,1)}, bf16[672,128]{1,0:T(8,128)(2,1)S(1)}, u32[]{:S(2)}) copy-start(bf16[672,128]{1,0:T(8,128)(2,1)S(1)} %collective-permute-done.8.refs_1_) | copy-start | bytes 516100
  50.3 0.8 %copy-start.6 = (bf16[864,128]{1,0:T(8,128)(2,1)}, bf16[864,128]{1,0:T(8,128)(2,1)S(1)}, u32[]{:S(2)}) copy-start(bf16[864,128]{1,0:T(8,128)(2,1)S(1)} %collective-permute-done.5.refs_0_) | copy-start | bytes 663556
  50.3 0.9 %copy-start.5 = (bf16[1536,128]{1,0:T(8,128)(2,1)}, bf16[1536,128]{1,0:T(8,128)(2,1)S(1)}, u32[]{:S(2)}) copy-start(bf16[1536,128]{1,0:T(8,128)(2,1)S(1)} %collective-permute-done.10.refs_4_) | copy-start | bytes 1179652

commit v4 on v3

--- a/solution.py
+++ b/solution.py
@@ -6,6 +6,7 @@
 from jax.experimental import pallas as pl
 from jax.experimental.pallas import tpu as pltpu
 from jax.sharding import PartitionSpec as P
+
 
 DENOM = 256
 TB_DEV = 64
@@ -137,6 +138,7 @@
         return pl.pallas_call(
             functools.partial(divide_kernel, part_levels=part_levels, field_vars=field_vars),
             out_shape=jax.ShapeDtypeStruct(shape, jnp.bfloat16),
+            compiler_params=pltpu.CompilerParams(vmem_limit_bytes=16 << 20),
             name="divide",
         )(*halves, *parts)
     parts = [p[:unit] for p in parts] + [jnp.concatenate(halves, axis=0)]
@@ -226,10 +228,14 @@
         away = wider(from_core[k][unit:][half])
         return wider(sums[4 * k + 2][half]) + jnp.where(for_column, zero, away)
 
-    column_sent = [
-        [lax.ppermute(narrower(column_part(k, half)), "narrow", back[k]) for k in range(1, groups)]
-        for half in halves
-    ]
+    column_sent = []
+    for half in halves:
+        column_sent.append(
+            [
+                lax.ppermute(narrower(column_part(k, half)), "narrow", back[k])
+                for k in range(1, groups)
+            ]
+        )
     other_side = [
         lax.ppermute(narrower(side_part(k, slice(0, unit))), "wide", to_side)
         for k in range(1, groups)
@@ -244,10 +250,10 @@
     for k in range(1, groups):
         total = wider(sums[4 * k + 3]) + wider(from_core[k][:unit]) + wider(other_side[k - 1])
         from_narrow.append(lax.ppermute(narrower(total), "narrow", back[k]))
-    from_side = [
-        lax.ppermute(narrower(side_part(0, half) + wider(piece)), "wide", to_side)
-        for half, piece in zip(halves, from_column)
-    ]
+    from_side = []
+    for half, piece in zip(halves, from_column):
+        part = narrower(side_part(0, half) + wider(piece))
+        from_side.append(lax.ppermute(part, "wide", to_side))
     final = [sums[3], from_core[0]] + from_narrow
     return divided(final, from_side, part_levels, field_vars, rows, in_kernel)
 

time: 54 us -> 50.9 us (0.943)
  local copies, waits for them, and re-layouts: 6.03 us -> 4.42 us
  Pallas kernels: 8.82 us -> 7.31 us
    unnamed x16 -> x6, local copies, waits for them, and re-layouts: 5.15 us -> 3.54 us
    pallas_call x1, Pallas kernels: 2.47 us -> 0.96 us  [divided(): pl.pallas_call(functools.partial(divide_kernel, part_levels=part_levels,...]
  transfers between devices with their start and end apart: 11 -> 11, of which waited for: 5 -> 5; matrix products, arithmetic and copies ran while one was open for 10% -> 11% of each run, Pallas kernels for 0% -> 0%
where the time goes in v4:
time: 50.9 us; the launch traced here: 50.5 us
  starting transfers between devices  19.7 us (39%)
  waiting for transfers between devices  12.9 us (25%)
  Pallas kernels  7.31 us (14%)
  other arithmetic  5.38 us (11%)
  local copies, waits for them, and re-layouts  4.42 us (9%)
  between operations  0.7 us (1%)
    ppermute x2, starting transfers between devices, per_device(): from_column.append(lax.ppermute(narrower(column), 'wide', to_column))  8 us
    ppermute x2, waiting for transfers between devices, per_device(): from_side.append(lax.ppermute(part, 'wide', to_side))  7.58 us
    pallas_call x1, Pallas kernels, pair_sums(): pl.pallas_call(functools.partial(sum_kernel, groups=groups, part_levels=p...  6.35 us
    convert_element_type x8, other arithmetic, per_device(): narrower = lambda a: a.astype(jnp.bfloat16)  4.67 us
    unnamed x6, local copies, waits for them, and re-layouts  3.54 us
    ppermute x1, starting transfers between devices, per_device(): lax.ppermute(piece, 'narrow', [(i, (i + k) % groups) for i in range(group...  3.03 us
    ppermute x2, starting transfers between devices, per_device(): from_side.append(lax.ppermute(part, 'wide', to_side))  2.39 us
    ppermute x2, starting transfers between devices, per_device(): lax.ppermute(narrower(column_part(k, half)), 'narrow', back[k])  2.17 us
  transfers between devices with their start and end apart: 11, of which 5 were waited for; matrix products, arithmetic and copies ran while one was open for 11% of the time, Pallas kernels for 0%

profile of v4, /device:TPU:0, one launch (start us, length us, event | category | flops | bytes accessed | tf_op | source)
XLA Modules:
  0.0 50.5 jit_solution(11661748981451480496)
XLA Ops:
  0.0 0.9 %constant_dynamic-slice_fusion = (bf16[2,8,2048]{2,1,0:T(8,128)(2,1)S(1)}, bf16[2,8,2048]{2,1,0:T(8,128)(2,1)S(1)}) fusion(bf16[2,8,4096]{2,1,0:T(8,128)(2,1)} %param.6, s32[]{:T(128)S(6)} %select_n.142, s32[]{:T(128)S(6)} %select_n.140), kind=kLoop, calls=%fused_computation.46 | loop fusion | bytes 262152 | tf_op jit(solution)/shard_map/dynamic_slice | solution.py:170
  0.9 3.0 %collective-permute-start = (bf16[2,8,2048]{2,1,0:T(8,128)(2,1)S(1)}, bf16[2,8,2048]{2,1,0:T(8,128)(2,1)S(1)}, u32[]{:S(2)}, u32[]{:S(2)}) collective-permute-start(bf16[2,8,2048]{2,1,0:T(8,128)(2,1)S(1)} %get-tuple-element.21), channel_id=1, source_target_pairs={{0,1},{1,0},{2,3},{3,2},{4,5},{5,4},{6,7},{7,6},{8,9},{9,8},{10,11... | collective-permute-start | bytes 196616 | tf_op jit(solution)/shard_map/ppermute | solution.py:172
  4.6 0.7 %compare_select_fusion.6.slot_ref = s32[128]{0:T(128)S(1)} fusion(s32[128]{0:T(128)} %param.10, s32[]{:T(128)S(6)} %select_n.131, s32[]{:T(128)S(6)} %select_n.128, s32[]{:T(128)S(6)} %select_n.126, s32[]{:T(128)} %bitcast.2), kind=kLoop, calls=%fused_computation.32 | loop fusion | flops 8064 | bytes 1040 | tf_op jit(solution)/shard_map/jit(_where)/select_n | solution.py:190
  5.3 0.9 %collective-permute-done.rest_1_ = bf16[2,8,2048]{2,1,0:T(8,128)(2,1)S(1)} collective-permute-done((bf16[2,8,2048]{2,1,0:T(8,128)(2,1)S(1)}, bf16[2,8,2048]{2,1,0:T(8,128)(2,1)S(1)}, u32[]{:S(2)}, u32[]{:S(2)}) %collective-permute-start) | collective-permute-done | bytes 65568 | tf_op jit(solution)/shard_map/ppermute | solution.py:172
  6.2 0.0 copy-start
  6.2 2.2 %copy-done = s32[128,64,128]{2,1,0:T(8,128)S(1)} copy-done((s32[128,64,128]{2,1,0:T(8,128)S(1)}, s32[128,64,128]{2,1,0:T(8,128)}, u32[]{:S(2)}) %copy-start) | copy-done | bytes 4194328
  8.4 0.0 copy-start.1
  8.4 0.7 %copy-done.1 = s32[2048]{0:T(1024)S(1)} copy-done((s32[2048]{0:T(1024)S(1)}, s32[2048]{0:T(1024)}, u32[]{:S(2)}) %copy-start.1) | copy-done | bytes 8216
  9.0 0.0 copy-start.2
  9.1 0.7 %copy-done.2 = s32[128]{0:T(128)S(1)} copy-done((s32[128]{0:T(128)S(1)}, s32[128]{0:T(128)}, u32[]{:S(2)}) %copy-start.2) | copy-done | bytes 536
  9.7 6.3 %pair_sums.1 = (bf16[3072,128]{1,0:T(8,128)(2,1)S(1)}, bf16[1536,128]{1,0:T(8,128)(2,1)S(1)}, bf16[1536,128]{1,0:T(8,128)(2,1)S(1)}, bf16[1536,128]{1,0:T(8,128)...) custom-call(s32[128]{0:T(128)S(1)} %copy-done.2, ...), custom_call_target="tpu_custom_call" | custom-call | tf_op jit(solution)/shard_map/pair_sums/pallas_call | solution.py:95
  16.1 0.0 collective-permute-start.2
  16.1 0.5 %collective-permute-start.1 = (bf16[3072,128]{1,0:T(8,128)(2,1)S(1)}, bf16[3072,128]{1,0:T(8,128)(2,1)S(1)}, u32[]{:S(2)}, u32[]{:S(2)}) collective-permute-start(bf16[3072,128]{1,0:T(8,128)(2,1)S(1)} %get-tuple-element.14), channel_id=1, source_target_pairs={{0,2},{2,0},{4,6},{6,4},{8,10},{10,8},{12,14},{14,12},{16,18},{18,... | collective-permute-start | bytes 2359304 | tf_op jit(solution)/shard_map/ppermute | solution.py:221
  16.6 2.1 %collective-permute-done.2 = bf16[3072,128]{1,0:T(8,128)(2,1)} collective-permute-done((bf16[3072,128]{1,0:T(8,128)(2,1)}, bf16[3072,128]{1,0:T(8,128)(2,1)}, u32[]{:S(2)}, u32[]{:S(2)}) %collective-permute-start.2) | collective-permute-done | bytes 786464 | tf_op jit(solution)/shard_map/ppermute | solution.py:221
  18.7 1.0 %add_convert_fusion.3 = bf16[672,128]{1,0:T(8,128)(2,1)S(1)} fusion(bf16[3072,128]{1,0:T(8,128)(2,1)} %collective-permute-done.2, bf16[1536,128]{1,0:T(8,128)(2,1)S(1)} %get-tuple-element.16, pred[]{:T(512)S(6)} %ne.83), kind=kLoop, calls=%fused_computation.19 | loop fusion | flops 430080 | bytes 516097 | tf_op jit(solution)/shard_map/convert_element_type | solution.py:217
  19.7 2.1 %collective-permute-start.6 = (bf16[672,128]{1,0:T(8,128)(2,1)S(1)}, bf16[672,128]{1,0:T(8,128)(2,1)S(1)}, u32[]{:S(2)}, u32[]{:S(2)}) collective-permute-start(bf16[672,128]{1,0:T(8,128)(2,1)S(1)} %add_convert_fusion.3), channel_id=1, source_target_pairs={{0,1},{1,0},{2,3},{3,2},{4,5},{5,4},{6,7},{7,6},{8,9},{9,8},{10,11... | collective-permute-start | bytes 516104 | tf_op jit(solution)/shard_map/ppermute | solution.py:235
  21.8 1.0 %add_convert_fusion.2 = bf16[864,128]{1,0:T(8,128)(2,1)S(1)} fusion(bf16[3072,128]{1,0:T(8,128)(2,1)} %collective-permute-done.2, bf16[1536,128]{1,0:T(8,128)(2,1)S(1)} %get-tuple-element.16, pred[]{:T(512)S(6)} %ne.83), kind=kLoop, calls=%fused_computation.10 | loop fusion | flops 552960 | bytes 663553 | tf_op jit(solution)/shard_map/convert_element_type | solution.py:217
  22.8 0.1 collective-permute-start.3
  22.8 1.1 %add_convert_fusion.1 = bf16[1536,128]{1,0:T(8,128)(2,1)S(1)} fusion(bf16[1536,128]{1,0:T(8,128)(2,1)S(1)} %get-tuple-element.20, bf16[3072,128]{1,0:T(8,128)(2,1)} %collective-permute-done.2, pred[]{:T(512)S(6)} %ne.83), kind=kLoop, calls=%fused_computation.1 | loop fusion | flops 983040 | bytes 1179649 | tf_op jit(solution)/shard_map/convert_element_type | solution.py:217
  24.0 2.1 %collective-permute-start.9 = (bf16[1536,128]{1,0:T(8,128)(2,1)S(1)}, bf16[1536,128]{1,0:T(8,128)(2,1)S(1)}, u32[]{:S(2)}, u32[]{:S(2)}) collective-permute-start(bf16[1536,128]{1,0:T(8,128)(2,1)S(1)} %add_convert_fusion.1), channel_id=1, source_target_pairs={{0,4},{2,6},{4,0},{6,2},{8,12},{10,14},{12,8},{14,10},{16,20},{18,... | collective-permute-start | bytes 1179656 | tf_op jit(solution)/shard_map/ppermute | solution.py:240
  26.1 0.0 collective-permute-done.1.refs_3_
  26.1 0.9 %collective-permute-done.6 = bf16[672,128]{1,0:T(8,128)(2,1)S(1)} collective-permute-done((bf16[672,128]{1,0:T(8,128)(2,1)S(1)}, bf16[672,128]{1,0:T(8,128)(2,1)S(1)}, u32[]{:S(2)}, u32[]{:S(2)}) %collective-permute-start.6) | collective-permute-done | bytes 172064 | tf_op jit(solution)/shard_map/ppermute | solution.py:235
  27.0 0.1 fusion.11
  27.1 4.2 %collective-permute-start.7 = (bf16[672,128]{1,0:T(8,128)(2,1)S(1)}, bf16[672,128]{1,0:T(8,128)(2,1)S(1)}, u32[]{:S(2)}, u32[]{:S(2)}) collective-permute-start(bf16[672,128]{1,0:T(8,128)(2,1)S(1)} %fusion.11), channel_id=1, source_target_pairs={{0,24},{2,26},{4,12},{6,14},{8,0},{10,2},{12,20},{14,22},{16,8},{1... | collective-permute-start | bytes 516104 | tf_op jit(solution)/shard_map/ppermute | solution.py:248
  31.3 0.0 collective-permute-done.3
  31.3 0.1 fusion.5
  31.4 3.8 %collective-permute-start.4 = (bf16[864,128]{1,0:T(8,128)(2,1)S(1)}, bf16[864,128]{1,0:T(8,128)(2,1)S(1)}, u32[]{:S(2)}, u32[]{:S(2)}) collective-permute-start(bf16[864,128]{1,0:T(8,128)(2,1)S(1)} %fusion.5), channel_id=1, source_target_pairs={{0,24},{2,26},{4,12},{6,14},{8,0},{10,2},{12,20},{14,22},{16,8},{1... | collective-permute-start | bytes 663560 | tf_op jit(solution)/shard_map/ppermute | solution.py:248
  35.2 0.0 collective-permute-done.9
  35.2 1.2 %add_convert_fusion = bf16[1536,128]{1,0:T(8,128)(2,1)S(1)} fusion(bf16[1536,128]{1,0:T(8,128)(2,1)S(1)} %collective-permute-done.9, bf16[1536,128]{1,0:T(8,128)(2,1)S(1)} %get-tuple-element.19, bf16[3072,128]{1,0:T(8,128)(2,1)} %collective-permute-done.2), kind=kLoop, calls=%fused_computation | loop fusion | flops 1179648 | bytes 1572864 | tf_op jit(solution)/shard_map/convert_element_type | solution.py:217
  36.4 1.5 %collective-permute-start.10 = (bf16[1536,128]{1,0:T(8,128)(2,1)S(1)}, bf16[1536,128]{1,0:T(8,128)(2,1)S(1)}, u32[]{:S(2)}, u32[]{:S(2)}) collective-permute-start(bf16[1536,128]{1,0:T(8,128)(2,1)S(1)} %add_convert_fusion), channel_id=1, source_target_pairs={{0,1},{1,0},{2,3},{3,2},{4,5},{5,4},{6,7},{7,6},{8,9},{9,8},{10,11... | collective-permute-start | bytes 1179656 | tf_op jit(solution)/shard_map/ppermute | solution.py:252
  37.9 1.4 %collective-permute-done.4 = bf16[864,128]{1,0:T(8,128)(2,1)S(1)} collective-permute-done((bf16[864,128]{1,0:T(8,128)(2,1)S(1)}, bf16[864,128]{1,0:T(8,128)(2,1)S(1)}, u32[]{:S(2)}, u32[]{:S(2)}) %collective-permute-start.4) | collective-permute-done | bytes 221216 | tf_op jit(solution)/shard_map/ppermute | solution.py:248
  39.3 0.1 fusion.2
  39.4 2.3 %collective-permute-start.5 = (bf16[864,128]{1,0:T(8,128)(2,1)S(1)}, bf16[864,128]{1,0:T(8,128)(2,1)S(1)}, u32[]{:S(2)}, u32[]{:S(2)}) collective-permute-start(bf16[864,128]{1,0:T(8,128)(2,1)S(1)} %fusion.2), channel_id=1, source_target_pairs={{0,4},{2,6},{4,0},{6,2},{8,12},{10,14},{12,8},{14,10},{16,20},{18,... | collective-permute-start | bytes 663560 | tf_op jit(solution)/shard_map/ppermute | solution.py:256
  41.7 0.0 collective-permute-done.7
  41.7 0.1 fusion.8
  41.8 0.1 collective-permute-start.8
  41.9 7.6 %collective-permute-done.8.refs_1_ = bf16[672,128]{1,0:T(8,128)(2,1)S(1)} collective-permute-done((bf16[672,128]{1,0:T(8,128)(2,1)S(1)}, bf16[672,128]{1,0:T(8,128)(2,1)S(1)}, u32[]{:S(2)}, u32[]{:S(2)}) %collective-permute-start.8) | collective-permute-done | bytes 172064 | tf_op jit(solution)/shard_map/ppermute | solution.py:256
  49.5 0.0 collective-permute-done.5.refs_0_
  49.5 0.0 collective-permute-done.10.refs_4_
  49.5 1.0 %divide.1 = bf16[2,8,8192]{2,1,0:T(8,128)(2,1)} custom-call(bf16[864,128]{1,0:T(8,128)(2,1)S(1)} %collective-permute-done.5.refs_0_, bf16[672,128]{1,0:T(8,128)(2,1)S(1)} %collective-permute-done.8.refs_1_, bf16[1536,128]{1,0:T(8,128)(2,1)S(1)} %get-tuple-element.18.refs_2_, bf16[3072,128]{1,0:T(8,128)(2,1)S(1)} %collective-permute-done.1.refs_3_, ...), custom_call_target="tpu_custom_call" | custom-call | tf_op jit(solution)/shard_map/divide/pallas_call | solution.py:138
  (1 shorter events, 0.0 us)
Async XLA Ops:
  0.9 5.3 %collective-permute-start = (bf16[2,8,2048]{2,1,0:T(8,128)(2,1)S(1)}, bf16[2,8,2048]{2,1,0:T(8,128)(2,1)S(1)}, u32[]{:S(2)}, u32[]{:S(2)}) collective-permute-start(bf16[2,8,2048]{2,1,0:T(8,128)(2,1)S(1)} %get-tuple-element.21), channel_id=1, source_target_pairs={{0,1},{1,0},{2,3},{3,2},{4,5},{5,4},{6,7},{7,6},{8,9},{9,8},{10,11... | collective-permute-start | bytes 196616 | tf_op jit(solution)/shard_map/ppermute | solution.py:172
  6.2 2.2 %copy-start = (s32[128,64,128]{2,1,0:T(8,128)S(1)}, s32[128,64,128]{2,1,0:T(8,128)}, u32[]{:S(2)}) copy-start(s32[128,64,128]{2,1,0:T(8,128)} %packed_ref.1) | copy-start | bytes 12582916
  8.4 0.7 %copy-start.1 = (s32[2048]{0:T(1024)S(1)}, s32[2048]{0:T(1024)}, u32[]{:S(2)}) copy-start(s32[2048]{0:T(1024)} %param.7) | copy-start | bytes 24580
  9.0 0.7 %copy-start.2 = (s32[128]{0:T(128)S(1)}, s32[128]{0:T(128)}, u32[]{:S(2)}) copy-start(s32[128]{0:T(128)} %source_ref.1) | copy-start | bytes 1540
  16.1 2.6 %collective-permute-start.2 = (bf16[3072,128]{1,0:T(8,128)(2,1)}, bf16[3072,128]{1,0:T(8,128)(2,1)}, u32[]{:S(2)}, u32[]{:S(2)}) collective-permute-start(bf16[3072,128]{1,0:T(8,128)(2,1)} %get-tuple-element.17), channel_id=1, source_target_pairs={{0,2},{2,0},{4,6},{6,4},{8,10},{10,8},{12,14},{14,12},{16,18},{18,... | collective-permute-start | bytes 2359304 | tf_op jit(solution)/shard_map/ppermute | solution.py:221
  16.1 10.0 %collective-permute-start.1 = (bf16[3072,128]{1,0:T(8,128)(2,1)S(1)}, bf16[3072,128]{1,0:T(8,128)(2,1)S(1)}, u32[]{:S(2)}, u32[]{:S(2)}) collective-permute-start(bf16[3072,128]{1,0:T(8,128)(2,1)S(1)} %get-tuple-element.14), channel_id=1, source_target_pairs={{0,2},{2,0},{4,6},{6,4},{8,10},{10,8},{12,14},{14,12},{16,18},{18,... | collective-permute-start | bytes 2359304 | tf_op jit(solution)/shard_map/ppermute | solution.py:221
  19.7 7.3 %collective-permute-start.6 = (bf16[672,128]{1,0:T(8,128)(2,1)S(1)}, bf16[672,128]{1,0:T(8,128)(2,1)S(1)}, u32[]{:S(2)}, u32[]{:S(2)}) collective-permute-start(bf16[672,128]{1,0:T(8,128)(2,1)S(1)} %add_convert_fusion.3), channel_id=1, source_target_pairs={{0,1},{1,0},{2,3},{3,2},{4,5},{5,4},{6,7},{7,6},{8,9},{9,8},{10,11... | collective-permute-start | bytes 516104 | tf_op jit(solution)/shard_map/ppermute | solution.py:235
  22.8 8.5 %collective-permute-start.3 = (bf16[864,128]{1,0:T(8,128)(2,1)S(1)}, bf16[864,128]{1,0:T(8,128)(2,1)S(1)}, u32[]{:S(2)}, u32[]{:S(2)}) collective-permute-start(bf16[864,128]{1,0:T(8,128)(2,1)S(1)} %add_convert_fusion.2), channel_id=1, source_target_pairs={{0,1},{1,0},{2,3},{3,2},{4,5},{5,4},{6,7},{7,6},{8,9},{9,8},{10,11... | collective-permute-start | bytes 663560 | tf_op jit(solution)/shard_map/ppermute | solution.py:235
  24.0 11.2 %collective-permute-start.9 = (bf16[1536,128]{1,0:T(8,128)(2,1)S(1)}, bf16[1536,128]{1,0:T(8,128)(2,1)S(1)}, u32[]{:S(2)}, u32[]{:S(2)}) collective-permute-start(bf16[1536,128]{1,0:T(8,128)(2,1)S(1)} %add_convert_fusion.1), channel_id=1, source_target_pairs={{0,4},{2,6},{4,0},{6,2},{8,12},{10,14},{12,8},{14,10},{16,20},{18,... | collective-permute-start | bytes 1179656 | tf_op jit(solution)/shard_map/ppermute | solution.py:240
  27.1 14.7 %collective-permute-start.7 = (bf16[672,128]{1,0:T(8,128)(2,1)S(1)}, bf16[672,128]{1,0:T(8,128)(2,1)S(1)}, u32[]{:S(2)}, u32[]{:S(2)}) collective-permute-start(bf16[672,128]{1,0:T(8,128)(2,1)S(1)} %fusion.11), channel_id=1, source_target_pairs={{0,24},{2,26},{4,12},{6,14},{8,0},{10,2},{12,20},{14,22},{16,8},{1... | collective-permute-start | bytes 516104 | tf_op jit(solution)/shard_map/ppermute | solution.py:248
  31.4 7.9 %collective-permute-start.4 = (bf16[864,128]{1,0:T(8,128)(2,1)S(1)}, bf16[864,128]{1,0:T(8,128)(2,1)S(1)}, u32[]{:S(2)}, u32[]{:S(2)}) collective-permute-start(bf16[864,128]{1,0:T(8,128)(2,1)S(1)} %fusion.5), channel_id=1, source_target_pairs={{0,24},{2,26},{4,12},{6,14},{8,0},{10,2},{12,20},{14,22},{16,8},{1... | collective-permute-start | bytes 663560 | tf_op jit(solution)/shard_map/ppermute | solution.py:248
  36.4 13.2 %collective-permute-start.10 = (bf16[1536,128]{1,0:T(8,128)(2,1)S(1)}, bf16[1536,128]{1,0:T(8,128)(2,1)S(1)}, u32[]{:S(2)}, u32[]{:S(2)}) collective-permute-start(bf16[1536,128]{1,0:T(8,128)(2,1)S(1)} %add_convert_fusion), channel_id=1, source_target_pairs={{0,1},{1,0},{2,3},{3,2},{4,5},{5,4},{6,7},{7,6},{8,9},{9,8},{10,11... | collective-permute-start | bytes 1179656 | tf_op jit(solution)/shard_map/ppermute | solution.py:252
  39.4 10.1 %collective-permute-start.5 = (bf16[864,128]{1,0:T(8,128)(2,1)S(1)}, bf16[864,128]{1,0:T(8,128)(2,1)S(1)}, u32[]{:S(2)}, u32[]{:S(2)}) collective-permute-start(bf16[864,128]{1,0:T(8,128)(2,1)S(1)} %fusion.2), channel_id=1, source_target_pairs={{0,4},{2,6},{4,0},{6,2},{8,12},{10,14},{12,8},{14,10},{16,20},{18,... | collective-permute-start | bytes 663560 | tf_op jit(solution)/shard_map/ppermute | solution.py:256
  41.8 7.7 %collective-permute-start.8 = (bf16[672,128]{1,0:T(8,128)(2,1)S(1)}, bf16[672,128]{1,0:T(8,128)(2,1)S(1)}, u32[]{:S(2)}, u32[]{:S(2)}) collective-permute-start(bf16[672,128]{1,0:T(8,128)(2,1)S(1)} %fusion.8), channel_id=1, source_target_pairs={{0,4},{2,6},{4,0},{6,2},{8,12},{10,14},{12,8},{14,10},{16,20},{18,... | collective-permute-start | bytes 516104 | tf_op jit(solution)/shard_map/ppermute | solution.py:256
